TPU v7x, 32 devices: a whole 2x2x4 slice. The times are simulated.
32 devices in a mesh: depth: 8 (over z, core), tile: 4 (over y, x).
Axes of the slice: x: 2, y: 2, z: 4, core: 2. Of those that a mesh axis runs over, the one named last changes fastest.
Arguments:
- potential: float32 [8, 1024, 384], P('depth', 'tile'), may hold values from 0 to 3
- probe: bfloat16 [2, 256, 256], replicated, may hold values from -6 to 6
- positions: int32 [4, 19, 2], P('tile'), may hold values from 0 to 128
- intensity: bfloat16 [4, 4, 256, 256], P('tile'), may hold values from 0.099609375 to 3
- fwd_wave: float32 [8, 4, 2, 256, 256], P('depth', 'tile'), may hold values from -6 to 6
- adj_wave: bfloat16 [8, 4, 2, 256, 256], P('depth', 'tile'), may hold values from -6 to 6
- saved_wave: bfloat16 [8, 4, 4, 2, 256, 256], P('depth', 'tile'), may hold values from -6 to 6
Outputs:
- fwd_next: float32 [8, 4, 2, 256, 256], P('depth', 'tile')
- adj_next: bfloat16 [8, 4, 2, 256, 256], P('depth', 'tile')
- gradient: float32 [8, 1024, 384], P('depth', 'tile')
Inputs may be any that keep to these rules, and one draw needn't show every extreme that they name: `positions`: window corners keep the whole window inside the tile's extent.
All inputs are finite; a program needn't handle non-finite values.
Results may differ from a plain program's by a relative error of at most 0.04.
Values may be sent and summed in bfloat16 or wider, within the bound.
A program may use at most 64 MiB of HBM per device.

v0:
```python
import functools
import math

import jax
import jax.numpy as jnp
import numpy as np
from jax import lax
from jax.experimental import pallas as pl
from jax.experimental.pallas import tpu as pltpu
from jax.sharding import PartitionSpec as P

SIGMA = 0.8
DEFOCUS = 6.0
ROWS = 128
STEP = 32
VLIM = 55
MESH = pl.DeviceIdType.MESH
F32 = jnp.float32
BF16 = jnp.bfloat16


def rounded(x):
    return x.real.astype(BF16).astype(np.float64) + 1j * x.imag.astype(BF16).astype(np.float64)


def tables(n):
    idx = np.arange(n)
    angle = (idx[:, None] * idx[None, :] % n) * (2.0 * math.pi / n)
    scale = 1.0 / math.sqrt(n)
    cos_t = np.asarray((np.cos(angle) * scale).astype(BF16)).astype(np.float64)
    sin_t = np.asarray((np.sin(angle) * scale).astype(BF16)).astype(np.float64)
    freq = np.where(idx < n // 2, idx, idx - n).astype(np.float64)
    q = np.exp(-1j * math.pi * DEFOCUS * freq * freq / (n * n))
    f = cos_t - 1j * sin_t
    m = (np.conj(f) * q[None, :]) @ f
    m = (m + m.T) / 2
    best = (np.inf, 1.0)
    for size in np.linspace(0.7, 1.4, 64):
        turns = size * np.exp(1j * np.linspace(0.0, math.pi / 2, 128, endpoint=False))
        row = m[0][None, :] / turns[:, None]
        miss = np.sum(np.abs(rounded(row) - row) ** 2, axis=1) * size * size
        at = int(np.argmin(miss))
        if miss[at] < best[0]:
            best = (miss[at], turns[at])
    z = best[1]
    near = rounded(z * m)
    rest = z * m - near
    g = np.conj(f) * q[None, :]
    parts = [x for v in (near, rest, m / z, f, g, g.T) for x in (v.real, v.imag)]
    return np.stack([p.astype(BF16) for p in parts])


def sin_cos(x):
    k = jnp.floor(x * (2.0 / math.pi) + 0.5)
    r = x - k * 1.5703125
    r = r - k * 4.837512969970703125e-4
    r = r - k * 7.54978995489188216e-8
    z = r * r
    s = r + r * z * (-1.6666654611e-1 + z * (8.3321608736e-3 + z * -1.9515295891e-4))
    c = 1.0 - 0.5 * z + z * z * (
        4.166664568298827e-2 + z * (-1.388731625493765e-3 + z * 2.443315711809948e-5)
    )
    half = jnp.floor(k * 0.5)
    odd = k - 2.0 * half > 0.5
    quarter = half - 2.0 * jnp.floor(half * 0.5)
    sign = 1.0 - 2.0 * quarter
    sin_v = jnp.where(odd, c, s) * sign
    cos_v = jnp.where(odd, -s, c) * sign
    return sin_v, cos_v


def dot(a, b):
    return jnp.dot(a, b, preferred_element_type=F32)


def kernel(
    sections, tiles,
    pos, pot_h, probe_h, inten_h, fwd_h, adj_h, saved_h, tab_h,
    o_fwd, o_adj, o_grad,
    in_f, in_b, out_f, out_b, l_f, m_f, r_f, l_b, m_b, r_b, l_g, r_g,
    ext, tf, ta, bk, total, a_buf, y_buf,
    halo_out, halo_in, edge_out, edge_in,
    pot, probe, inten, fwd, adj, saved, tab, load_sem,
    send_f, recv_f, send_b, recv_b, send_h, recv_h, send_e, recv_e,
):
    n = probe.shape[1]
    nc = n // ROWS
    core, width = pot.shape[1], pot.shape[2]
    margin = (width - core) // 2
    ticks = inten.shape[1]
    s = lax.axis_index("depth")
    t = lax.axis_index("tile")
    first, last = s == 0, s == sections - 1
    low, high = t == 0, t == tiles - 1

    loads = {}
    for i, (name, src, dst) in enumerate((
        ("pot", pot_h, pot), ("tab", tab_h, tab), ("adj", adj_h, adj), ("fwd", fwd_h, fwd),
        ("probe", probe_h, probe), ("saved", saved_h, saved), ("inten", inten_h, inten),
    )):
        loads[name] = pltpu.make_async_copy(src, dst, load_sem.at[i])
        loads[name].start()

    barrier = pltpu.get_barrier_semaphore()
    one = lambda c: jnp.where(c, 1, 0).astype(jnp.int32)

    def greet(cond, axis, to):
        @pl.when(cond)
        def _():
            pl.semaphore_signal(barrier, inc=1, device_id={axis: to}, device_id_type=MESH)

    greet(s > 0, "depth", s - 1)
    greet(s < sections - 1, "depth", s + 1)
    greet(t > 0, "tile", t - 1)
    greet(t < tiles - 1, "tile", t + 1)
    loads["pot"].wait()
    halo_out[0] = pot[0, 0:margin, :].astype(BF16)
    halo_out[1] = pot[0, core - margin : core, :].astype(BF16)
    pl.semaphore_wait(barrier, one(s > 0) + one(s < sections - 1) + one(t > 0) + one(t < tiles - 1))

    def hop(src, dst, ssem, rsem, axis, to):
        return pltpu.make_async_remote_copy(
            src_ref=src, dst_ref=dst, send_sem=ssem, recv_sem=rsem,
            device_id={axis: to}, device_id_type=MESH,
        )

    def tile_pair(src, dst, ssem, rsem):
        down = hop(src.at[0], dst.at[1], ssem.at[0], rsem.at[1], "tile", t - 1)
        up = hop(src.at[1], dst.at[0], ssem.at[1], rsem.at[0], "tile", t + 1)
        return down, up

    def tile_start(src, dst, ssem, rsem):
        down, up = tile_pair(src, dst, ssem, rsem)
        pl.when(t > 0)(down.start)
        pl.when(t < tiles - 1)(up.start)

    def tile_wait(src, dst, ssem, rsem):
        down, up = tile_pair(src, dst, ssem, rsem)

        @pl.when(t > 0)
        def _():
            down.wait_send()
            up.wait_recv()

        @pl.when(t < tiles - 1)
        def _():
            up.wait_send()
            down.wait_recv()

    tile_start(halo_out, halo_in, send_h, recv_h)

    def fill_left(ref, lr, li):
        for c in range(nc):
            cols = slice(c * ROWS, (c + 1) * ROWS)
            ref[c, 0:n, 0:ROWS] = lr[:, cols]
            ref[c, 0:n, ROWS : 2 * ROWS] = -li[:, cols]
            ref[c, n : 2 * n, 0:ROWS] = li[:, cols]
            ref[c, n : 2 * n, ROWS : 2 * ROWS] = lr[:, cols]

    def fill_right(ref, rr, ri):
        ref[0:n, 0:n] = rr
        ref[0:n, n : 2 * n] = ri
        ref[n : 2 * n, 0:n] = -ri
        ref[n : 2 * n, n : 2 * n] = rr

    loads["tab"].wait()
    fill_left(l_b, tab[0], -tab[1])
    fill_left(m_b, tab[2], -tab[3])
    fill_right(r_b, tab[4], -tab[5])

    @pl.when(jnp.logical_not(last))
    def _():
        fill_left(l_f, tab[0], tab[1])
        fill_left(m_f, tab[2], tab[3])
        fill_right(r_f, tab[4], tab[5])

    @pl.when(last)
    def _():
        fill_left(l_f, tab[6], tab[7])
        m_f[...] = jnp.zeros_like(m_f)
        fill_right(r_f, tab[6], tab[7])
        fill_left(l_g, tab[8], tab[9])
        fill_right(r_g, tab[10], tab[11])

    for name in ("adj", "fwd", "probe"):
        loads[name].wait()
    for c in range(nc):
        for part in range(2):
            rows = slice(c * ROWS, (c + 1) * ROWS)
            to = slice(part * ROWS, (part + 1) * ROWS)
            in_f[0, c, to, :] = fwd[0, 0, part, rows, :].astype(BF16)
            in_b[0, c, to, :] = adj[0, 0, part, rows, :]

    @pl.when(first)
    def _():
        for k in range(ticks):
            for c in range(nc):
                in_f[k + 1, c] = jnp.concatenate(
                    [probe[part, c * ROWS : (c + 1) * ROWS, :] for part in range(2)], axis=0
                )

    total[...] = jnp.zeros_like(total)
    ext[margin : margin + core, :] = pot[0].astype(BF16)

    @pl.when(low)
    def _():
        halo_in[0] = jnp.zeros((margin, width), BF16)
        edge_in[0] = jnp.zeros((margin, width), BF16)

    @pl.when(high)
    def _():
        halo_in[1] = jnp.zeros((margin, width), BF16)
        edge_in[1] = jnp.zeros((margin, width), BF16)

    tile_wait(halo_out, halo_in, send_h, recv_h)
    ext[0:margin, :] = halo_in[0]
    ext[margin + core :, :] = halo_in[1]

    def chosen(offset, axis):
        shape = (n, width) if axis else (width, n)
        ahead = lax.broadcasted_iota(jnp.int32, shape, axis) - lax.broadcasted_iota(
            jnp.int32, shape, 1 - axis
        )
        return jnp.where(ahead == offset, 1.0, 0.0).astype(BF16)

    def window(index, out):
        rows = dot(chosen(pos[0, 0, index], 1), ext[...]).astype(BF16)
        bk[0] = SIGMA * dot(rows, chosen(pos[0, 1, index], 0))
        for at in range(0, n, STEP):
            sv, cv = sin_cos(bk[0, at : at + STEP, :])
            out[0, at : at + STEP, :] = cv
            out[1, at : at + STEP, :] = sv

    def copy_f(k, c):
        return hop(out_f.at[k, c], in_f.at[k + 1, c], send_f.at[k, c], recv_f.at[k, c], "depth", s + 1)

    def copy_b(k, c):
        return hop(out_b.at[k, c], in_b.at[k + 1, c], send_b.at[k, c], recv_b.at[k, c], "depth", s - 1)

    def right(r_ref, c):
        rows = slice(c * ROWS, (c + 1) * ROWS)
        more = slice(n + c * ROWS, n + (c + 1) * ROWS)
        return dot(jnp.concatenate([a_buf[rows, :], a_buf[more, :]], axis=1), r_ref[...])

    def backward(k):
        acc = None
        for c in range(nc):
            @pl.when(jnp.logical_and(k > 0, jnp.logical_not(last)))
            def _():
                copy_b(k - 1, c).wait_recv()
            term = dot(l_b[c], in_b[k, c]) + dot(m_b[c], in_b[k, c])
            acc = term if acc is None else acc + term
        a_buf[...] = acc.astype(BF16)
        for c in range(nc):
            rows = slice(c * ROWS, (c + 1) * ROWS)
            lu = right(r_b, c)
            lur, lui = lu[:, 0:n], lu[:, n : 2 * n]
            tr, ti = ta[0, rows, :], ta[1, rows, :]
            br = tr * lur + ti * lui
            bi = tr * lui - ti * lur
            bk[0, rows, :] = br
            bk[1, rows, :] = bi
            out_b[k, c, 0:ROWS, :] = br.astype(BF16)
            out_b[k, c, ROWS : 2 * ROWS, :] = bi.astype(BF16)

            @pl.when(jnp.logical_not(first))
            def _():
                copy_b(k, c).start()

    def forward(k):
        acc = None
        for c in range(nc):
            rows = slice(c * ROWS, (c + 1) * ROWS)

            @pl.when(jnp.logical_and(k > 0, jnp.logical_not(first)))
            def _():
                copy_f(k - 1, c).wait_recv()
            wr = in_f[k, c, 0:ROWS, :].astype(F32)
            wi = in_f[k, c, ROWS : 2 * ROWS, :].astype(F32)
            tr, ti = tf[0, rows, :], tf[1, rows, :]
            u = jnp.concatenate([tr * wr - ti * wi, tr * wi + ti * wr], axis=0).astype(BF16)
            term = dot(l_f[c], u) + dot(m_f[c], u)
            acc = term if acc is None else acc + term
        a_buf[...] = acc.astype(BF16)

        @pl.when(jnp.logical_not(last))
        def _():
            for c in range(nc):
                out = right(r_f, c)
                out_f[k, c, 0:ROWS, :] = out[:, 0:n].astype(BF16)
                out_f[k, c, ROWS : 2 * ROWS, :] = out[:, n : 2 * n].astype(BF16)
                copy_f(k, c).start()

        @pl.when(last)
        def _():
            for c in range(nc):
                rows = slice(c * ROWS, (c + 1) * ROWS)
                out = right(r_f, c)
                vr, vi = out[:, 0:n], out[:, n : 2 * n]
                excess = vr * vr + vi * vi - inten[0, k, rows, :].astype(F32)
                y_buf[c, 0:ROWS, :] = (excess * vr).astype(BF16)
                y_buf[c, ROWS : 2 * ROWS, :] = (excess * vi).astype(BF16)
            left = None
            for c in range(nc):
                term = dot(l_g[c], y_buf[c])
                left = term if left is None else left + term
            a_buf[...] = left.astype(BF16)
            for c in range(nc):
                out = right(r_g, c)
                in_b[k + 1, c, 0:ROWS, :] = out[:, 0:n].astype(BF16)
                in_b[k + 1, c, ROWS : 2 * ROWS, :] = out[:, n : 2 * n].astype(BF16)

    early = jnp.logical_or(first, jnp.logical_and(lax.rem(s, 2) == 1, jnp.logical_not(last)))

    def tick(k, carry):
        window(k + s, ta)
        window(k - s + 2 * sections - 1, tf)

        @pl.when(early)
        def _():
            forward(k)

        backward(k)

        @pl.when(jnp.logical_not(early))
        def _():
            forward(k)

        sr = saved[0, 0, k, 0].astype(F32)
        si = saved[0, 0, k, 1].astype(F32)
        delta = SIGMA * (bk[1] * sr - bk[0] * si)
        coarse = delta.astype(BF16)
        fine = (delta - coarse.astype(F32)).astype(BF16)
        tall = dot(chosen(pos[0, 0, k + s], 0), jnp.concatenate([coarse, fine], axis=1)).astype(BF16)
        across = chosen(pos[0, 1, k + s], 1)
        total[...] += dot(tall[:, 0:n], across) + dot(tall[:, n : 2 * n], across)
        return carry

    for name in ("saved", "inten"):
        loads[name].wait()
    lax.fori_loop(0, ticks, tick, 0)

    edge_out[0] = total[0:margin, :].astype(BF16)
    edge_out[1] = total[margin + core :, :].astype(BF16)
    tile_start(edge_out, edge_in, send_e, recv_e)
    o_grad[0, margin : core - margin, :] = total[2 * margin : core, :]
    tile_wait(edge_out, edge_in, send_e, recv_e)
    o_grad[0, 0:margin, :] = total[margin : 2 * margin, :] + edge_in[0].astype(F32)
    o_grad[0, core - margin : core, :] = total[core : core + margin, :] + edge_in[1].astype(F32)
    for c in range(nc):
        rows = slice(c * ROWS, (c + 1) * ROWS)

        @pl.when(jnp.logical_not(last))
        def _():
            copy_b(ticks - 1, c).wait_recv()
        o_adj[0, 0, 0, rows, :] = in_b[ticks, c, 0:ROWS, :]
        o_adj[0, 0, 1, rows, :] = in_b[ticks, c, ROWS : 2 * ROWS, :]

        @pl.when(jnp.logical_not(first))
        def _():
            copy_f(ticks - 1, c).wait_recv()
        o_fwd[0, 0, 0, rows, :] = in_f[ticks, c, 0:ROWS, :]
        o_fwd[0, 0, 1, rows, :] = in_f[ticks, c, ROWS : 2 * ROWS, :]
    for k in range(ticks):
        for c in range(nc):
            @pl.when(jnp.logical_not(last))
            def _():
                copy_f(k, c).wait_send()

            @pl.when(jnp.logical_not(first))
            def _():
                copy_b(k, c).wait_send()


def on_device(sections, tiles, potential, probe, positions, intensity, fwd_wave, adj_wave, saved_wave):
    n = probe.shape[1]
    nc = n // ROWS
    ticks = intensity.shape[1]
    core, width = potential.shape[1], potential.shape[2]
    margin = (width - core) // 2
    tab = jnp.asarray(tables(n))
    held = lambda x: pltpu.VMEM(x.shape, x.dtype)
    vmem = pl.BlockSpec(memory_space=pltpu.VMEM)
    smem = pl.BlockSpec(memory_space=pltpu.SMEM)
    dma = lambda *shape: pltpu.SemaphoreType.DMA(shape)
    wave = lambda count: pltpu.VMEM((count, nc, 2 * ROWS, n), BF16)
    lt = pltpu.VMEM((nc, 2 * n, 2 * ROWS), BF16)
    rt = pltpu.VMEM((2 * n, 2 * n), BF16)
    two = pltpu.VMEM((2, n, n), F32)
    strip = pltpu.VMEM((2, margin, width), BF16)
    wave_next, adj_next, gradient = pl.pallas_call(
        functools.partial(kernel, sections, tiles),
        out_shape=(
            jax.ShapeDtypeStruct(fwd_wave.shape, BF16),
            jax.ShapeDtypeStruct(adj_wave.shape, BF16),
            jax.ShapeDtypeStruct(potential.shape, F32),
        ),
        in_specs=[smem] + [pl.BlockSpec(memory_space=pltpu.HBM)] * 7,
        out_specs=(vmem, vmem, vmem),
        scratch_shapes=[
            wave(ticks + 1), wave(ticks + 1), wave(ticks), wave(ticks),
            lt, lt, rt, lt, lt, rt, lt, rt,
            pltpu.VMEM((width, width), BF16), two, two, two,
            pltpu.VMEM((width, width), F32),
            pltpu.VMEM((2 * n, n), BF16),
            pltpu.VMEM((nc, 2 * ROWS, n), BF16),
            strip, strip, strip, strip,
            held(potential), held(probe), held(intensity), held(fwd_wave), held(adj_wave),
            held(saved_wave), held(tab), dma(7),
            dma(ticks, nc), dma(ticks, nc), dma(ticks, nc), dma(ticks, nc),
            dma(2), dma(2), dma(2), dma(2),
        ],
        compiler_params=pltpu.CompilerParams(
            collective_id=0, has_side_effects=True, vmem_limit_bytes=VLIM * 1024 * 1024
        ),
        name="window",
    )(jnp.swapaxes(positions, 1, 2), potential, probe, intensity, fwd_wave, adj_wave, saved_wave, tab)
    return wave_next.astype(F32), adj_next, gradient


def solution(mesh):
    placed = (
        P("depth", "tile", None),
        P(),
        P("tile", None, None),
        P("tile", None, None, None),
        P("depth", "tile", None, None, None),
        P("depth", "tile", None, None, None),
        P("depth", "tile", None, None, None, None),
    )
    return jax.shard_map(
        functools.partial(on_device, mesh.shape["depth"], mesh.shape["tile"]),
        mesh=mesh,
        in_specs=placed,
        out_specs=(
            P("depth", "tile", None, None, None),
            P("depth", "tile", None, None, None),
            P("depth", "tile", None),
        ),
        check_vma=False,
    )
```

profile of v0, /device:TPU:1, one launch (start us, length us, event | category | flops | bytes accessed | tf_op | source)
XLA Modules:
  0.0 34.6 jit_solution(12538695987463019887)
XLA Ops:
  0.6 29.7 %window.1 = (bf16[1,1,2,256,256]{4,3,2,1,0:T(8,128)(2,1)}, bf16[1,1,2,256,256]{4,3,2,1,0:T(8,128)(2,1)}, f32[1,256,384]{2,1,0:T(8,128)}) custom-call(s32[1,2,19]{2,1,0:T(2,128)} %bitcast.1, f32[1,256,384]{2,1,0:T(8,128)} %pot_h.1, bf16[2,256,256]{2,1,0:T(8,128)(2,1)} %probe_h.1, bf16[1,4,256,256]{3,2,1,0:T(8,128)(2,1)} %inten_h.1, ...), custom_call_target="tpu_custom_call" | custom-call | tf_op jit(solution)/shard_map/window/pallas_call | solution.py:391
  30.4 0.0 copy-start
  30.4 1.8 %convert_element_type.3 = f32[1,1,2,256,256]{4,3,2,1,0:T(8,128)} convert(bf16[1,1,2,256,256]{4,3,2,1,0:T(8,128)(2,1)} %get-tuple-element.6) | non-fusion elementwise | flops 131072 | bytes 786432 | tf_op jit(solution)/shard_map/convert_element_type | solution.py:418
  32.2 1.7 %copy.13 = bf16[1,1,2,256,256]{4,3,2,1,0:T(8,128)(2,1)} copy(bf16[1,1,2,256,256]{4,3,2,1,0:T(8,128)(2,1)} %get-tuple-element.13) | data formatting | bytes 524288
  33.9 0.0 copy-done
  33.9 0.7 %copy.14 = f32[1,256,384]{2,1,0:T(8,128)} copy(f32[1,256,384]{2,1,0:T(8,128)S(1)} %copy-done) | data formatting | bytes 786432
Async XLA Ops:
  30.4 3.5 %copy-start = (f32[1,256,384]{2,1,0:T(8,128)S(1)}, f32[1,256,384]{2,1,0:T(8,128)}, u32[]{:S(2)}) copy-start(f32[1,256,384]{2,1,0:T(8,128)} %get-tuple-element.14) | copy-start | bytes 1179652
where the time goes:
time: 35.2 us; the launch traced here: 34.6 us
  Pallas kernels  29.7 us (84%)
  local copies, waits for them, and re-layouts  2.42 us (7%)
  other arithmetic  1.83 us (5%)
  between operations  0.65 us (2%)
    pallas_call x1, Pallas kernels, on_device(): pl.pallas_call(functools.partial(kernel, sections, tiles), out_shape=(jax...  29.7 us
    unnamed x4, local copies, waits for them, and re-layouts  2.42 us
    convert_element_type x1, other arithmetic, on_device(): return (wave_next.astype(F32), adj_next, gradient)  1.83 us

commit v1 on v0

v1 whole, which is shorter than its diff:
```python
import functools
import math

import jax
import jax.numpy as jnp
import numpy as np
from jax import lax
from jax.experimental import pallas as pl
from jax.experimental.pallas import tpu as pltpu
from jax.sharding import PartitionSpec as P

SIGMA = 0.8
DEFOCUS = 6.0
VTOP = 3.0
ROWS = 128
LANES = 128
STEP = 32
VLIM = 40
MESH = pl.DeviceIdType.MESH
F32 = jnp.float32
BF16 = jnp.bfloat16


def rounded(x):
    return x.real.astype(BF16).astype(np.float64) + 1j * x.imag.astype(BF16).astype(np.float64)


def left_blocks(x):
    n = x.shape[0]
    nc = n // ROWS
    out = np.zeros((nc, nc, 2 * ROWS, 2 * ROWS))
    for o in range(nc):
        for c in range(nc):
            b = x[o * ROWS : (o + 1) * ROWS, c * ROWS : (c + 1) * ROWS]
            out[o, c] = np.block([[b.real, -b.imag], [b.imag, b.real]])
    return out.transpose(0, 2, 1, 3).reshape(2 * n, 2 * n)


def right_block(x):
    return np.block([[x.real, x.imag], [-x.imag, x.real]])


def tables(n):
    idx = np.arange(n)
    angle = (idx[:, None] * idx[None, :] % n) * (2.0 * math.pi / n)
    scale = 1.0 / math.sqrt(n)
    cos_t = np.asarray((np.cos(angle) * scale).astype(BF16)).astype(np.float64)
    sin_t = np.asarray((np.sin(angle) * scale).astype(BF16)).astype(np.float64)
    freq = np.where(idx < n // 2, idx, idx - n).astype(np.float64)
    q = np.exp(-1j * math.pi * DEFOCUS * freq * freq / (n * n))
    f = cos_t - 1j * sin_t
    m = (np.conj(f) * q[None, :]) @ f
    m = (m + m.T) / 2
    best = (np.inf, 1.0)
    for size in np.linspace(0.7, 1.4, 64):
        z = (size * np.exp(1j * np.linspace(0.0, math.pi / 2, 128, endpoint=False)))[:, None]
        row = m[0][None, :]
        miss = np.sum(np.abs(rounded(row * z) - row * z) ** 2, axis=1) / size**2
        miss += np.sum(np.abs(rounded(row / z) - row / z) ** 2, axis=1) * size**2
        at = int(np.argmin(miss))
        if miss[at] < best[0]:
            best = (miss[at], z[at, 0])
    z = best[1]
    g = np.conj(f) * q[None, :]
    main = np.stack([left_blocks(z * m), right_block(m / z)]).astype(BF16)
    ends = [p for v in (f, g, g.T) for p in (v.real, v.imag)]
    return main, np.stack(ends).astype(BF16)


def sin_cos(v):
    mid = 0.5 * VTOP * SIGMA
    y = v * SIGMA - mid
    z = y * y
    s = y * (1.0 + z * (-1.0 / 6 + z * (1.0 / 120 + z * (-1.0 / 5040 + z * (1.0 / 362880)))))
    c = 1.0 + z * (-0.5 + z * (1.0 / 24 + z * (-1.0 / 720 + z * (1.0 / 40320))))
    sm, cm = math.sin(mid), math.cos(mid)
    return s * cm + c * sm, c * cm - s * sm


def dot(a, b):
    return jnp.dot(a, b, preferred_element_type=F32)


def kernel(
    sections, tiles,
    pos, pot_h, probe_h, inten_h, fwd_h, adj_h, saved_h, main_h, ends_h,
    o_fwd, o_adj, o_grad,
    in_f, in_b, out_f, out_b, main, l_f, r_f, l_g, r_g,
    cs, tf, ta, bk, total, pad, y_buf,
    halo_out, halo_in, edge_out, edge_in,
    pot, probe, inten, fwd, adj, saved, ends, load_sem,
    send_f, recv_f, send_b, recv_b, send_h, recv_h, send_e, recv_e,
):
    n = probe.shape[1]
    nc = n // ROWS
    cols = n // LANES
    core, width = pot.shape[1], pot.shape[2]
    margin = (width - core) // 2
    ticks = inten.shape[1]
    s = lax.axis_index("depth")
    t = lax.axis_index("tile")
    first, last = s == 0, s == sections - 1
    low, high = t == 0, t == tiles - 1

    loads = {}

    def load(name, src, dst):
        loads[name] = pltpu.make_async_copy(src, dst, load_sem.at[len(loads)])
        return loads[name]

    load("pot", pot_h, pot).start()
    barrier = pltpu.get_barrier_semaphore()
    one = lambda c: jnp.where(c, 1, 0).astype(jnp.int32)

    def greet(cond, axis, to):
        @pl.when(cond)
        def _():
            pl.semaphore_signal(barrier, inc=1, device_id={axis: to}, device_id_type=MESH)

    greet(t > 0, "tile", t - 1)
    greet(t < tiles - 1, "tile", t + 1)
    greet(s > 0, "depth", s - 1)
    greet(s < sections - 1, "depth", s + 1)
    load("main", main_h, main).start()
    load("adj", adj_h, adj).start()
    load("fwd", fwd_h, fwd).start()
    load("probe", probe_h, probe)
    load("ends", ends_h, ends)
    load("inten", inten_h, inten)

    @pl.when(first)
    def _():
        loads["probe"].start()

    @pl.when(last)
    def _():
        loads["ends"].start()
        loads["inten"].start()

    load("saved", saved_h, saved).start()
    loads["pot"].wait()
    halo_out[0] = pot[0, 0:margin, :].astype(BF16)
    halo_out[1] = pot[0, core - margin : core, :].astype(BF16)
    pl.semaphore_wait(barrier, one(s > 0) + one(s < sections - 1) + one(t > 0) + one(t < tiles - 1))

    def hop(src, dst, ssem, rsem, axis, to):
        return pltpu.make_async_remote_copy(
            src_ref=src, dst_ref=dst, send_sem=ssem, recv_sem=rsem,
            device_id={axis: to}, device_id_type=MESH,
        )

    def tile_pair(src, dst, ssem, rsem):
        down = hop(src.at[0], dst.at[1], ssem.at[0], rsem.at[1], "tile", t - 1)
        up = hop(src.at[1], dst.at[0], ssem.at[1], rsem.at[0], "tile", t + 1)
        return down, up

    def tile_start(src, dst, ssem, rsem):
        down, up = tile_pair(src, dst, ssem, rsem)
        pl.when(t > 0)(down.start)
        pl.when(t < tiles - 1)(up.start)

    def tile_wait(src, dst, ssem, rsem):
        down, up = tile_pair(src, dst, ssem, rsem)

        @pl.when(t > 0)
        def _():
            down.wait_send()
            up.wait_recv()

        @pl.when(t < tiles - 1)
        def _():
            up.wait_send()
            down.wait_recv()

    tile_start(halo_out, halo_in, send_h, recv_h)

    def stacked(x):
        return x.reshape(2 * ROWS, n)

    def m_left(o, c):
        return main[0, o * 2 * ROWS : (o + 1) * 2 * ROWS, c * 2 * ROWS : (c + 1) * 2 * ROWS]

    def product(get_left, get_x, r_ref, sink):
        acc = [None] * nc
        for c in range(nc):
            x = get_x(c)
            for o in range(nc):
                term = dot(get_left(o, c), x)
                acc[o] = term if acc[o] is None else acc[o] + term
        for o in range(nc):
            a = acc[o].astype(BF16)
            out = dot(jnp.concatenate([a[0:ROWS, :], a[ROWS : 2 * ROWS, :]], axis=1), r_ref[...])
            sink(o, out[:, 0:n], out[:, n : 2 * n])

    loads["adj"].wait()
    for c in range(nc):
        rows = slice(c * ROWS, (c + 1) * ROWS)
        in_b[0, c, 0] = adj[0, 0, 0, rows, :]
        in_b[0, c, 1] = -adj[0, 0, 1, rows, :]
    loads["main"].wait()

    def keep(o, lur, lui):
        rows = slice(o * ROWS, (o + 1) * ROWS)
        bk[0, rows, :] = lur
        bk[1, rows, :] = lui

    product(m_left, lambda c: stacked(in_b[0, c]), main.at[1], keep)

    def table(src, dst, count):
        for at in range(0, count, STEP):
            sv, cv = sin_cos(src(at))
            for i in range(cols + 1):
                one_tile = slice(i * LANES, (i + 1) * LANES)
                cs[i, pl.ds(2 * (dst + at), STEP, stride=2), :] = cv[:, one_tile]
                cs[i, pl.ds(2 * (dst + at) + 1, STEP, stride=2), :] = sv[:, one_tile]

    table(lambda at: pot[0, at : at + STEP, :], margin, core)
    total[...] = jnp.zeros_like(total)
    spare = width - n
    for i in range(cols + 1):
        pad[i, 0 : 2 * spare, :] = jnp.zeros((2 * spare, LANES), F32)
        pad[i, 2 * (spare + n) :, :] = jnp.zeros((2 * spare, LANES), F32)
    loads["fwd"].wait()
    for c in range(nc):
        rows = slice(c * ROWS, (c + 1) * ROWS)
        for part in range(2):
            in_f[0, c, part] = fwd[0, 0, part, rows, :].astype(BF16)

    @pl.when(first)
    def _():
        loads["probe"].wait()
        for k in range(ticks - 1):
            for c in range(nc):
                for part in range(2):
                    in_f[k + 1, c, part] = probe[part, c * ROWS : (c + 1) * ROWS, :]
        for part in range(2):
            o_fwd[0, 0, part] = probe[part]

    @pl.when(last)
    def _():
        loads["ends"].wait()
        loads["inten"].wait()

        def fill_left(ref, xr, xi):
            for o in range(nc):
                for c in range(nc):
                    br = xr[o * ROWS : (o + 1) * ROWS, c * ROWS : (c + 1) * ROWS]
                    bi = xi[o * ROWS : (o + 1) * ROWS, c * ROWS : (c + 1) * ROWS]
                    ref[o, c, 0:ROWS, 0:ROWS] = br
                    ref[o, c, 0:ROWS, ROWS : 2 * ROWS] = -bi
                    ref[o, c, ROWS : 2 * ROWS, 0:ROWS] = bi
                    ref[o, c, ROWS : 2 * ROWS, ROWS : 2 * ROWS] = br

        def fill_right(ref, xr, xi):
            ref[0:n, 0:n] = xr
            ref[0:n, n : 2 * n] = xi
            ref[n : 2 * n, 0:n] = -xi
            ref[n : 2 * n, n : 2 * n] = xr

        fill_left(l_f, ends[0], ends[1])
        fill_right(r_f, ends[0], ends[1])
        fill_left(l_g, ends[2], ends[3])
        fill_right(r_g, ends[4], ends[5])

    @pl.when(low)
    def _():
        halo_in[0] = jnp.zeros((margin, width), BF16)
        edge_in[0] = jnp.zeros((margin, width), BF16)

    @pl.when(high)
    def _():
        halo_in[1] = jnp.zeros((margin, width), BF16)
        edge_in[1] = jnp.zeros((margin, width), BF16)

    tile_wait(halo_out, halo_in, send_h, recv_h)
    table(lambda at: halo_in[0, at : at + STEP, :].astype(F32), 0, margin)
    table(lambda at: halo_in[1, at : at + STEP, :].astype(F32), margin + core, margin)

    lane = lax.broadcasted_iota(jnp.int32, (STEP, LANES), 1)

    def window(index, out, slot):
        r, c = pos[0, 0, index], pos[0, 1, index]
        turn = lax.rem(LANES - c, LANES)
        own = lane < LANES - c
        for part in range(2):
            for at in range(0, n, STEP):
                rows = pl.ds(2 * (r + at) + part, STEP, stride=2)
                x = [pltpu.roll(cs[i, rows, :], turn, 1) for i in range(cols + 1)]
                for i in range(cols):
                    out[slot, part, at : at + STEP, i * LANES : (i + 1) * LANES] = jnp.where(own, x[i], x[i + 1])

    def windows(k):
        window(k + s, ta, lax.rem(k, 2))
        window(k - s + 2 * sections - 1, tf, lax.rem(k, 2))

    def scatter(k):
        r, c = pos[0, 0, k + s], pos[0, 1, k + s]
        own = lane >= c
        turn = lax.rem(c, LANES)
        for at in range(0, n, STEP):
            rows = slice(at, at + STEP)
            sr = saved[0, 0, k, 0, rows, :].astype(F32)
            si = saved[0, 0, k, 1, rows, :].astype(F32)
            d = (bk[1, rows, :] * sr + bk[0, rows, :] * si) * -SIGMA
            d = [pltpu.roll(d[:, i * LANES : (i + 1) * LANES], turn, 1) for i in range(cols)]
            zero = jnp.zeros((STEP, LANES), F32)
            d = [zero] + d + [zero]
            for i in range(cols + 1):
                pad[i, pl.ds(2 * (spare + at), STEP, stride=2), :] = jnp.where(own, d[i + 1], d[i])
        for at in range(0, width, STEP):
            for i in range(cols + 1):
                total[at : at + STEP, i * LANES : (i + 1) * LANES] += pad[i, pl.ds(2 * (spare - r + at), STEP, stride=2), :]

    def copy_f(k, c):
        return hop(out_f.at[k, c], in_f.at[k + 1, c], send_f.at[k, c], recv_f.at[k, c], "depth", s + 1)

    def copy_b(k, c):
        return hop(out_b.at[k, c], in_b.at[k + 1, c], send_b.at[k, c], recv_b.at[k, c], "depth", s - 1)

    def send_back(k, c, lur, lui):
        rows = slice(c * ROWS, (c + 1) * ROWS)
        slot = lax.rem(k, 2)
        tr, ti = ta[slot, 0, rows, :], ta[slot, 1, rows, :]
        br = tr * lur - ti * lui
        bi = tr * lui + ti * lur
        bk[0, rows, :] = br
        bk[1, rows, :] = bi
        out_b[k, c, 0] = br.astype(BF16)
        out_b[k, c, 1] = bi.astype(BF16)

        @pl.when(jnp.logical_not(first))
        def _():
            copy_b(k, c).start()

    def backward(k):
        def arrived(c):
            @pl.when(jnp.logical_not(last))
            def _():
                copy_b(k - 1, c).wait_recv()
            return stacked(in_b[k, c])

        product(m_left, arrived, main.at[1], functools.partial(send_back, k))

    def entering(k, c, waits):
        if waits:
            @pl.when(jnp.logical_not(first))
            def _():
                copy_f(k - 1, c).wait_recv()
        rows = slice(c * ROWS, (c + 1) * ROWS)
        slot = lax.rem(k, 2)
        wr, wi = in_f[k, c, 0].astype(F32), in_f[k, c, 1].astype(F32)
        tr, ti = tf[slot, 0, rows, :], tf[slot, 1, rows, :]
        return jnp.concatenate([tr * wr - ti * wi, tr * wi + ti * wr], axis=0).astype(BF16)

    def forward(k, waits=True):
        def sink(c, outr, outi):
            out_f[k, c, 0] = outr.astype(BF16)
            out_f[k, c, 1] = outi.astype(BF16)
            copy_f(k, c).start()

        product(m_left, lambda c: entering(k, c, waits), main.at[1], sink)

    def forward_last(k, waits=True):
        def detect(c, vr, vi):
            rows = slice(c * ROWS, (c + 1) * ROWS)
            excess = vr * vr + vi * vi - inten[0, k, rows, :].astype(F32)
            y_buf[c, 0:ROWS, :] = (excess * vr).astype(BF16)
            y_buf[c, ROWS : 2 * ROWS, :] = (excess * vi).astype(BF16)

        def seed(c, outr, outi):
            in_b[k + 1, c, 0] = outr.astype(BF16)
            in_b[k + 1, c, 1] = -outi.astype(BF16)

        product(lambda o, c: l_f[o, c], lambda c: entering(k, c, waits), r_f, detect)
        product(lambda o, c: l_g[o, c], lambda c: y_buf[c], r_g, seed)

    windows(0)
    for c in range(nc):
        rows = slice(c * ROWS, (c + 1) * ROWS)
        send_back(0, c, bk[0, rows, :], bk[1, rows, :])

    @pl.when(jnp.logical_not(last))
    def _():
        forward(0, False)

    @pl.when(last)
    def _():
        forward_last(0, False)

    windows(1)
    loads["saved"].wait()
    scatter(0)

    early = jnp.logical_or(first, jnp.logical_and(lax.rem(s, 2) == 1, jnp.logical_not(last)))

    @pl.when(early)
    def _():
        def tick(k, carry):
            forward(k)

            @pl.when(k < ticks - 1)
            def _():
                windows(k + 1)
            backward(k)
            scatter(k)
            return carry
        lax.fori_loop(1, ticks, tick, 0)

    @pl.when(jnp.logical_not(early))
    def _():
        def tick(k, carry):
            backward(k)
            scatter(k)

            @pl.when(k < ticks - 1)
            def _():
                windows(k + 1)

            @pl.when(jnp.logical_not(last))
            def _():
                forward(k)

            @pl.when(last)
            def _():
                forward_last(k)
            return carry
        lax.fori_loop(1, ticks, tick, 0)

    edge_out[0] = total[0:margin, :].astype(BF16)
    edge_out[1] = total[margin + core :, :].astype(BF16)
    tile_start(edge_out, edge_in, send_e, recv_e)
    o_grad[0, margin : core - margin, :] = total[2 * margin : core, :]
    tile_wait(edge_out, edge_in, send_e, recv_e)
    o_grad[0, 0:margin, :] = total[margin : 2 * margin, :] + edge_in[0].astype(F32)
    o_grad[0, core - margin : core, :] = total[core : core + margin, :] + edge_in[1].astype(F32)
    for c in range(nc):
        rows = slice(c * ROWS, (c + 1) * ROWS)

        @pl.when(jnp.logical_not(last))
        def _():
            copy_b(ticks - 1, c).wait_recv()
        o_adj[0, 0, :, rows, :] = in_b[ticks, c]

        @pl.when(jnp.logical_not(first))
        def _():
            copy_f(ticks - 1, c).wait_recv()
            o_fwd[0, 0, :, rows, :] = in_f[ticks, c]
    for k in range(ticks):
        for c in range(nc):
            @pl.when(jnp.logical_not(last))
            def _():
                copy_f(k, c).wait_send()

            @pl.when(jnp.logical_not(first))
            def _():
                copy_b(k, c).wait_send()


def finish(wave, adj, grad, o_wave, o_adj, o_grad, wave_buf, adj_buf, sem):
    moves = [pltpu.make_async_copy(grad, o_grad, sem.at[0])]
    moves[0].start()
    for part in range(2):
        wave_buf[0, 0, part] = wave[0, 0, part].astype(F32)
        move = pltpu.make_async_copy(wave_buf.at[0, 0, part], o_wave.at[0, 0, part], sem.at[1 + part])
        move.start()
        moves.append(move)
    adj_buf[0, 0, 0] = adj[0, 0, 0]
    adj_buf[0, 0, 1] = -adj[0, 0, 1]
    moves.append(pltpu.make_async_copy(adj_buf, o_adj, sem.at[3]))
    moves[-1].start()
    for move in moves:
        move.wait()


def on_device(sections, tiles, potential, probe, positions, intensity, fwd_wave, adj_wave, saved_wave):
    n = probe.shape[1]
    nc = n // ROWS
    ticks = intensity.shape[1]
    core, width = potential.shape[1], potential.shape[2]
    margin = (width - core) // 2
    main, ends = (jnp.asarray(x) for x in tables(n))
    held = lambda x: pltpu.VMEM(x.shape, x.dtype)
    vmem = pl.BlockSpec(memory_space=pltpu.VMEM)
    smem = pl.BlockSpec(memory_space=pltpu.SMEM)
    hbm = pl.BlockSpec(memory_space=pltpu.HBM)
    dma = lambda *shape: pltpu.SemaphoreType.DMA(shape)
    wave = lambda count: pltpu.VMEM((count, nc, 2, ROWS, n), BF16)
    lt = pltpu.VMEM((nc, nc, 2 * ROWS, 2 * ROWS), BF16)
    rt = pltpu.VMEM((2 * n, 2 * n), BF16)
    square = pltpu.VMEM((width, width), F32)
    pair = pltpu.VMEM((2, 2, n, n), F32)
    strip = pltpu.VMEM((2, margin, width), BF16)
    wave_next, adj_next, gradient = pl.pallas_call(
        functools.partial(kernel, sections, tiles),
        out_shape=(
            pltpu.VMEM(fwd_wave.shape, BF16),
            pltpu.VMEM(adj_wave.shape, BF16),
            pltpu.VMEM(potential.shape, F32),
        ),
        in_specs=[smem] + [hbm] * 8,
        out_specs=(vmem, vmem, vmem),
        scratch_shapes=[
            wave(ticks + 1), wave(ticks + 1), wave(ticks), wave(ticks),
            held(main), lt, rt, lt, rt,
            pltpu.VMEM((width // LANES, 2 * width, LANES), F32), pair, pair, pltpu.VMEM((2, n, n), F32),
            square, pltpu.VMEM((width // LANES, 4 * width - 2 * n, LANES), F32),
            pltpu.VMEM((nc, 2 * ROWS, n), BF16),
            strip, strip, strip, strip,
            held(potential), held(probe), held(intensity), held(fwd_wave), held(adj_wave),
            held(saved_wave), held(ends), dma(8),
            dma(ticks, nc), dma(ticks, nc), dma(ticks, nc), dma(ticks, nc),
            dma(2), dma(2), dma(2), dma(2),
        ],
        compiler_params=pltpu.CompilerParams(
            collective_id=0, has_side_effects=True, vmem_limit_bytes=VLIM * 1024 * 1024
        ),
        name="window",
    )(jnp.swapaxes(positions, 1, 2), potential, probe, intensity, fwd_wave, adj_wave, saved_wave, main, ends)
    return pl.pallas_call(
        finish,
        out_shape=(
            jax.ShapeDtypeStruct(fwd_wave.shape, F32),
            jax.ShapeDtypeStruct(adj_wave.shape, BF16),
            jax.ShapeDtypeStruct(potential.shape, F32),
        ),
        in_specs=[vmem, vmem, vmem],
        out_specs=(hbm, hbm, hbm),
        scratch_shapes=[pltpu.VMEM(fwd_wave.shape, F32), held(adj_wave), dma(4)],
        name="finish",
    )(wave_next, adj_next, gradient)


def solution(mesh):
    placed = (
        P("depth", "tile", None),
        P(),
        P("tile", None, None),
        P("tile", None, None, None),
        P("depth", "tile", None, None, None),
        P("depth", "tile", None, None, None),
        P("depth", "tile", None, None, None, None),
    )
    return jax.shard_map(
        functools.partial(on_device, mesh.shape["depth"], mesh.shape["tile"]),
        mesh=mesh,
        in_specs=placed,
        out_specs=(
            P("depth", "tile", None, None, None),
            P("depth", "tile", None, None, None),
            P("depth", "tile", None),
        ),
        check_vma=False,
    )
```

time: 35.2 us -> 40.5 us (1.15)
  local copies, waits for them, and re-layouts: 2.42 us -> 11.4 us
  other arithmetic: 1.83 us -> 0 us
  Pallas kernels: 29.7 us -> 28 us
    unnamed x4 -> x24, local copies, waits for them, and re-layouts: 2.42 us -> 11.4 us
    convert_element_type x1 -> x0, other arithmetic: 1.83 us -> none  [on_device(): return (wave_next.astype(F32), adj_next, gradient)]
    pallas_call x1 -> x2, Pallas kernels: 29.7 us -> 28 us  [the longest x1 25.8 us: on_device(): pl.pallas_call(functools.partial(kernel, sections, tiles), out_shape=(plt...]
where the time goes in v1:
time: 40.5 us; the launch traced here: 40.1 us
  Pallas kernels  28 us (69%)
  local copies, waits for them, and re-layouts  11.4 us (28%)
  between operations  0.67 us (2%)
    pallas_call x1, Pallas kernels, on_device(): pl.pallas_call(functools.partial(kernel, sections, tiles), out_shape=(plt...  25.8 us
    unnamed x24, local copies, waits for them, and re-layouts  11.4 us
    pallas_call x1, Pallas kernels, on_device(): pl.pallas_call(finish, out_shape=(jax.ShapeDtypeStruct(fwd_wave.shape, F3...  2.19 us

profile of v1, /device:TPU:1, one launch (start us, length us, event | category | flops | bytes accessed | tf_op | source)
XLA Modules:
  0.0 40.1 jit_solution(5940156624270314985)
XLA Ops:
  0.6 0.0 copy-start.11
  0.6 0.7 %copy-done.11 = s32[1,19,2]{1,2,0:T(2,128)S(1)} copy-done((s32[1,19,2]{1,2,0:T(2,128)S(1)}, s32[1,19,2]{1,2,0:T(2,128)}, u32[]{:S(2)}) %copy-start.11) | copy-done | bytes 176
  1.3 0.0 copy-start
  1.3 1.2 %copy-done = bf16[1,1,4,2,256,256]{5,4,3,2,1,0:T(8,128)(2,1)S(1)} copy-done((bf16[1,1,4,2,256,256]{5,4,3,2,1,0:T(8,128)(2,1)S(1)}, bf16[1,1,4,2,256,256]{5,4,3,2,1,0:T(8,128)(2,1)}, u32[]{:S(2)}) %copy-start) | copy-done | bytes 1048600
  2.5 0.0 copy-start.1
  2.5 1.2 %copy-done.1 = bf16[2,512,512]{2,1,0:T(8,128)(2,1)S(1)} copy-done((bf16[2,512,512]{2,1,0:T(8,128)(2,1)S(1)}, bf16[2,512,512]{2,1,0:T(8,128)(2,1)}, u32[]{:S(2)}) %copy-start.1) | copy-done | bytes 1048600
  3.8 0.0 copy-start.2
  3.8 1.1 %copy-done.2 = bf16[6,256,256]{2,1,0:T(8,128)(2,1)S(1)} copy-done((bf16[6,256,256]{2,1,0:T(8,128)(2,1)S(1)}, bf16[6,256,256]{2,1,0:T(8,128)(2,1)}, u32[]{:S(2)}) %copy-start.2) | copy-done | bytes 786456
  4.9 0.0 copy-start.3
  4.9 1.0 %copy-done.3 = bf16[1,4,256,256]{3,2,1,0:T(8,128)(2,1)S(1)} copy-done((bf16[1,4,256,256]{3,2,1,0:T(8,128)(2,1)S(1)}, bf16[1,4,256,256]{3,2,1,0:T(8,128)(2,1)}, u32[]{:S(2)}) %copy-start.3) | copy-done | bytes 524312
  5.9 0.0 copy-start.4
  5.9 1.0 %copy-done.4 = f32[1,1,2,256,256]{4,3,2,1,0:T(8,128)S(1)} copy-done((f32[1,1,2,256,256]{4,3,2,1,0:T(8,128)S(1)}, f32[1,1,2,256,256]{4,3,2,1,0:T(8,128)}, u32[]{:S(2)}) %copy-start.4) | copy-done | bytes 524312
  7.0 0.0 copy-start.6
  7.0 1.0 %copy-done.6 = f32[1,256,384]{2,1,0:T(8,128)S(1)} copy-done((f32[1,256,384]{2,1,0:T(8,128)S(1)}, f32[1,256,384]{2,1,0:T(8,128)}, u32[]{:S(2)}) %copy-start.6) | copy-done | bytes 393240
  8.0 0.0 copy-start.9
  8.0 0.9 %copy-done.9 = bf16[2,256,256]{2,1,0:T(8,128)(2,1)S(1)} copy-done((bf16[2,256,256]{2,1,0:T(8,128)(2,1)S(1)}, bf16[2,256,256]{2,1,0:T(8,128)(2,1)}, u32[]{:S(2)}) %copy-start.9) | copy-done | bytes 262168
  8.9 0.0 copy-start.10
  8.9 0.9 %copy-done.10 = bf16[1,1,2,256,256]{4,3,2,1,0:T(8,128)(2,1)S(1)} copy-done((bf16[1,1,2,256,256]{4,3,2,1,0:T(8,128)(2,1)S(1)}, bf16[1,1,2,256,256]{4,3,2,1,0:T(8,128)(2,1)}, u32[]{:S(2)}) %copy-start.10) | copy-done | bytes 262168
  9.9 25.8 %window.1 = (bf16[1,1,2,256,256]{4,3,2,1,0:T(8,128)(2,1)S(1)}, bf16[1,1,2,256,256]{4,3,2,1,0:T(8,128)(2,1)S(1)}, f32[1,256,384]{2,1,0:T(8,128)S(1)}) custom-call(s32[1,2,19]{2,1,0:T(2,128)S(1)} %bitcast.1, f32[1,256,384]{2,1,0:T(8,128)S(1)} %copy-done.6, bf16[2,256,256]{2,1,0:T(8,128)(2,1)S(1)} %copy-done.9, bf16[1,4,256,256]{3,2,1,0:T(8,128)(2,1)S(1)} %copy-done.3, ...), custom_call_target="tpu_custom_call" | custom-call | tf_op jit(solution)/shard_map/window/pallas_call | solution.py:493
  35.7 0.0 copy-start.5
  35.7 0.7 %copy-done.5 = f32[1,256,384]{2,1,0:T(8,128)} copy-done((f32[1,256,384]{2,1,0:T(8,128)}, f32[1,256,384]{2,1,0:T(8,128)S(1)}, u32[]{:S(2)}) %copy-start.5) | copy-done | bytes 393240
  36.5 0.0 copy-start.7
  36.5 0.7 %copy-done.7 = bf16[1,1,2,256,256]{4,3,2,1,0:T(8,128)(2,1)} copy-done((bf16[1,1,2,256,256]{4,3,2,1,0:T(8,128)(2,1)}, bf16[1,1,2,256,256]{4,3,2,1,0:T(8,128)(2,1)S(1)}, u32[]{:S(2)}) %copy-start.7) | copy-done | bytes 262168
  37.2 0.0 copy-start.8
  37.2 0.7 %copy-done.8 = bf16[1,1,2,256,256]{4,3,2,1,0:T(8,128)(2,1)} copy-done((bf16[1,1,2,256,256]{4,3,2,1,0:T(8,128)(2,1)}, bf16[1,1,2,256,256]{4,3,2,1,0:T(8,128)(2,1)S(1)}, u32[]{:S(2)}) %copy-start.8) | copy-done | bytes 262168
  37.9 2.2 %finish.1 = (f32[1,1,2,256,256]{4,3,2,1,0:T(8,128)}, bf16[1,1,2,256,256]{4,3,2,1,0:T(8,128)(2,1)}, f32[1,256,384]{2,1,0:T(8,128)}) custom-call(bf16[1,1,2,256,256]{4,3,2,1,0:T(8,128)(2,1)} %copy-done.7, bf16[1,1,2,256,256]{4,3,2,1,0:T(8,128)(2,1)} %copy-done.8, f32[1,256,384]{2,1,0:T(8,128)} %copy-done.5), custom_call_target="tpu_custom_call" | custom-call | tf_op jit(solution)/shard_map/finish/pallas_call | solution.py:519
Async XLA Ops:
  0.6 0.7 %copy-start.11 = (s32[1,19,2]{1,2,0:T(2,128)S(1)}, s32[1,19,2]{1,2,0:T(2,128)}, u32[]{:S(2)}) copy-start(s32[1,19,2]{1,2,0:T(2,128)} %param.11) | copy-start | bytes 460
  1.3 1.2 %copy-start = (bf16[1,1,4,2,256,256]{5,4,3,2,1,0:T(8,128)(2,1)S(1)}, bf16[1,1,4,2,256,256]{5,4,3,2,1,0:T(8,128)(2,1)}, u32[]{:S(2)}) copy-start(bf16[1,1,4,2,256,256]{5,4,3,2,1,0:T(8,128)(2,1)} %saved_h.1) | copy-start | bytes 3145732
  2.5 1.2 %copy-start.1 = (bf16[2,512,512]{2,1,0:T(8,128)(2,1)S(1)}, bf16[2,512,512]{2,1,0:T(8,128)(2,1)}, u32[]{:S(2)}) copy-start(bf16[2,512,512]{2,1,0:T(8,128)(2,1)} %constant.4.clone.main_h) | copy-start | bytes 3145732
  3.8 1.1 %copy-start.2 = (bf16[6,256,256]{2,1,0:T(8,128)(2,1)S(1)}, bf16[6,256,256]{2,1,0:T(8,128)(2,1)}, u32[]{:S(2)}) copy-start(bf16[6,256,256]{2,1,0:T(8,128)(2,1)} %constant.5.clone.ends_h) | copy-start | bytes 2359300
  4.9 1.0 %copy-start.3 = (bf16[1,4,256,256]{3,2,1,0:T(8,128)(2,1)S(1)}, bf16[1,4,256,256]{3,2,1,0:T(8,128)(2,1)}, u32[]{:S(2)}) copy-start(bf16[1,4,256,256]{3,2,1,0:T(8,128)(2,1)} %inten_h.1) | copy-start | bytes 1572868
  5.9 1.0 %copy-start.4 = (f32[1,1,2,256,256]{4,3,2,1,0:T(8,128)S(1)}, f32[1,1,2,256,256]{4,3,2,1,0:T(8,128)}, u32[]{:S(2)}) copy-start(f32[1,1,2,256,256]{4,3,2,1,0:T(8,128)} %fwd_h.1) | copy-start | bytes 1572868
  7.0 1.0 %copy-start.6 = (f32[1,256,384]{2,1,0:T(8,128)S(1)}, f32[1,256,384]{2,1,0:T(8,128)}, u32[]{:S(2)}) copy-start(f32[1,256,384]{2,1,0:T(8,128)} %pot_h.1) | copy-start | bytes 1179652
  8.0 0.9 %copy-start.9 = (bf16[2,256,256]{2,1,0:T(8,128)(2,1)S(1)}, bf16[2,256,256]{2,1,0:T(8,128)(2,1)}, u32[]{:S(2)}) copy-start(bf16[2,256,256]{2,1,0:T(8,128)(2,1)} %probe_h.1) | copy-start | bytes 786436
  8.9 0.9 %copy-start.10 = (bf16[1,1,2,256,256]{4,3,2,1,0:T(8,128)(2,1)S(1)}, bf16[1,1,2,256,256]{4,3,2,1,0:T(8,128)(2,1)}, u32[]{:S(2)}) copy-start(bf16[1,1,2,256,256]{4,3,2,1,0:T(8,128)(2,1)} %adj_h.1) | copy-start | bytes 786436
  35.7 0.7 %copy-start.5 = (f32[1,256,384]{2,1,0:T(8,128)}, f32[1,256,384]{2,1,0:T(8,128)S(1)}, u32[]{:S(2)}) copy-start(f32[1,256,384]{2,1,0:T(8,128)S(1)} %get-tuple-element.8.grad) | copy-start | bytes 1179652
  36.5 0.7 %copy-start.7 = (bf16[1,1,2,256,256]{4,3,2,1,0:T(8,128)(2,1)}, bf16[1,1,2,256,256]{4,3,2,1,0:T(8,128)(2,1)S(1)}, u32[]{:S(2)}) copy-start(bf16[1,1,2,256,256]{4,3,2,1,0:T(8,128)(2,1)S(1)} %get-tuple-element.6.wave) | copy-start | bytes 786436
  37.2 0.7 %copy-start.8 = (bf16[1,1,2,256,256]{4,3,2,1,0:T(8,128)(2,1)}, bf16[1,1,2,256,256]{4,3,2,1,0:T(8,128)(2,1)S(1)}, u32[]{:S(2)}) copy-start(bf16[1,1,2,256,256]{4,3,2,1,0:T(8,128)(2,1)S(1)} %get-tuple-element.7.adj) | copy-start | bytes 786436

commit v2 on v1

--- a/solution.py
+++ b/solution.py
@@ -484,6 +484,8 @@
     smem = pl.BlockSpec(memory_space=pltpu.SMEM)
     hbm = pl.BlockSpec(memory_space=pltpu.HBM)
     dma = lambda *shape: pltpu.SemaphoreType.DMA(shape)
+    far = lambda x: pltpu.with_memory_space_constraint(x, pltpu.HBM)
+    near = lambda x: pltpu.with_memory_space_constraint(x, pltpu.VMEM)
     wave = lambda count: pltpu.VMEM((count, nc, 2, ROWS, n), BF16)
     lt = pltpu.VMEM((nc, nc, 2 * ROWS, 2 * ROWS), BF16)
     rt = pltpu.VMEM((2 * n, 2 * n), BF16)
@@ -515,7 +517,10 @@
             collective_id=0, has_side_effects=True, vmem_limit_bytes=VLIM * 1024 * 1024
         ),
         name="window",
-    )(jnp.swapaxes(positions, 1, 2), potential, probe, intensity, fwd_wave, adj_wave, saved_wave, main, ends)
+    )(
+        far(jnp.swapaxes(positions, 1, 2)),
+        *(far(x) for x in (potential, probe, intensity, fwd_wave, adj_wave, saved_wave, main, ends)),
+    )
     return pl.pallas_call(
         finish,
         out_shape=(
@@ -527,7 +532,7 @@
         out_specs=(hbm, hbm, hbm),
         scratch_shapes=[pltpu.VMEM(fwd_wave.shape, F32), held(adj_wave), dma(4)],
         name="finish",
-    )(wave_next, adj_next, gradient)
+    )(near(wave_next), near(adj_next), near(gradient))
 
 
 def solution(mesh):

time: 40.5 us -> 27.7 us (0.68)
  local copies, waits for them, and re-layouts: 11.4 us -> 0 us
  Pallas kernels: 28 us -> 26.9 us
    unnamed x24 -> x0, local copies, waits for them, and re-layouts: 11.4 us -> none
    pallas_call x1, Pallas kernels: 2.19 us -> 1.04 us  [on_device(): pl.pallas_call(finish, out_shape=(jax.ShapeDtypeStruct(fwd_wave.shape, F3...]
where the time goes in v2:
time: 27.7 us; the launch traced here: 27.5 us
  Pallas kernels  26.9 us (97%)
  between operations  0.64 us (2%)
    pallas_call x1, Pallas kernels, on_device(): pl.pallas_call(functools.partial(kernel, sections, tiles), out_shape=(plt...  25.8 us
    pallas_call x1, Pallas kernels, on_device(): pl.pallas_call(finish, out_shape=(jax.ShapeDtypeStruct(fwd_wave.shape, F3...  1.04 us

profile of v2, /device:TPU:1, one launch (start us, length us, event | category | flops | bytes accessed | tf_op | source)
XLA Modules:
  0.0 27.5 jit_solution(30762530239863819)
XLA Ops:
  0.6 25.8 %window.1 = (bf16[1,1,2,256,256]{4,3,2,1,0:T(8,128)(2,1)S(1)}, bf16[1,1,2,256,256]{4,3,2,1,0:T(8,128)(2,1)S(1)}, f32[1,256,384]{2,1,0:T(8,128)S(1)}) custom-call(s32[1,2,19]{2,1,0:T(2,128)} %bitcast.1, f32[1,256,384]{2,1,0:T(8,128)} %pot_h.1, bf16[2,256,256]{2,1,0:T(8,128)(2,1)} %probe_h.1, bf16[1,4,256,256]{3,2,1,0:T(8,128)(2,1)} %inten_h.1, ...), custom_call_target="tpu_custom_call" | custom-call | tf_op jit(solution)/shard_map/window/pallas_call | solution.py:495
  26.5 1.0 %finish.1 = (f32[1,1,2,256,256]{4,3,2,1,0:T(8,128)}, bf16[1,1,2,256,256]{4,3,2,1,0:T(8,128)(2,1)}, f32[1,256,384]{2,1,0:T(8,128)}) custom-call(bf16[1,1,2,256,256]{4,3,2,1,0:T(8,128)(2,1)S(1)} %get-tuple-element.6.wave, bf16[1,1,2,256,256]{4,3,2,1,0:T(8,128)(2,1)S(1)} %get-tuple-element.7.adj, f32[1,256,384]{2,1,0:T(8,128)S(1)} %get-tuple-element.8.grad), custom_call_target="tpu_custom_call" | custom-call | tf_op jit(solution)/shard_map/finish/pallas_call | solution.py:524

commit v3 on v2

--- a/solution.py
+++ b/solution.py
@@ -83,12 +83,12 @@
 
 def kernel(
     sections, tiles,
-    pos, pot_h, probe_h, inten_h, fwd_h, adj_h, saved_h, main_h, ends_h,
+    pos_h, pot_h, probe_h, inten_h, fwd_h, adj_h, saved_h, main_h, ends_h,
     o_fwd, o_adj, o_grad,
     in_f, in_b, out_f, out_b, main, l_f, r_f, l_g, r_g,
     cs, tf, ta, bk, total, pad, y_buf,
     halo_out, halo_in, edge_out, edge_in,
-    pot, probe, inten, fwd, adj, saved, ends, load_sem,
+    pos, pot, probe, inten, fwd, adj, saved, ends, load_sem,
     send_f, recv_f, send_b, recv_b, send_h, recv_h, send_e, recv_e,
 ):
     n = probe.shape[1]
@@ -108,7 +108,6 @@
         loads[name] = pltpu.make_async_copy(src, dst, load_sem.at[len(loads)])
         return loads[name]
 
-    load("pot", pot_h, pot).start()
     barrier = pltpu.get_barrier_semaphore()
     one = lambda c: jnp.where(c, 1, 0).astype(jnp.int32)
 
@@ -121,6 +120,8 @@
     greet(t < tiles - 1, "tile", t + 1)
     greet(s > 0, "depth", s - 1)
     greet(s < sections - 1, "depth", s + 1)
+    load("pot", pot_h, pot).start()
+    load("pos", pos_h, pos).start()
     load("main", main_h, main).start()
     load("adj", adj_h, adj).start()
     load("fwd", fwd_h, fwd).start()
@@ -374,6 +375,7 @@
         product(lambda o, c: l_f[o, c], lambda c: entering(k, c, waits), r_f, detect)
         product(lambda o, c: l_g[o, c], lambda c: y_buf[c], r_g, seed)
 
+    loads["pos"].wait()
     windows(0)
     for c in range(nc):
         rows = slice(c * ROWS, (c + 1) * ROWS)
@@ -481,7 +483,7 @@
     main, ends = (jnp.asarray(x) for x in tables(n))
     held = lambda x: pltpu.VMEM(x.shape, x.dtype)
     vmem = pl.BlockSpec(memory_space=pltpu.VMEM)
-    smem = pl.BlockSpec(memory_space=pltpu.SMEM)
+    spots = jnp.swapaxes(positions, 1, 2)
     hbm = pl.BlockSpec(memory_space=pltpu.HBM)
     dma = lambda *shape: pltpu.SemaphoreType.DMA(shape)
     far = lambda x: pltpu.with_memory_space_constraint(x, pltpu.HBM)
@@ -499,7 +501,7 @@
             pltpu.VMEM(adj_wave.shape, BF16),
             pltpu.VMEM(potential.shape, F32),
         ),
-        in_specs=[smem] + [hbm] * 8,
+        in_specs=[hbm] * 9,
         out_specs=(vmem, vmem, vmem),
         scratch_shapes=[
             wave(ticks + 1), wave(ticks + 1), wave(ticks), wave(ticks),
@@ -508,8 +510,8 @@
             square, pltpu.VMEM((width // LANES, 4 * width - 2 * n, LANES), F32),
             pltpu.VMEM((nc, 2 * ROWS, n), BF16),
             strip, strip, strip, strip,
-            held(potential), held(probe), held(intensity), held(fwd_wave), held(adj_wave),
-            held(saved_wave), held(ends), dma(8),
+            pltpu.SMEM(spots.shape, spots.dtype), held(potential), held(probe), held(intensity), held(fwd_wave), held(adj_wave),
+            held(saved_wave), held(ends), dma(9),
             dma(ticks, nc), dma(ticks, nc), dma(ticks, nc), dma(ticks, nc),
             dma(2), dma(2), dma(2), dma(2),
         ],
@@ -518,8 +520,7 @@
         ),
         name="window",
     )(
-        far(jnp.swapaxes(positions, 1, 2)),
-        *(far(x) for x in (potential, probe, intensity, fwd_wave, adj_wave, saved_wave, main, ends)),
+        *(far(x) for x in (spots, potential, probe, intensity, fwd_wave, adj_wave, saved_wave, main, ends)),
     )
     return pl.pallas_call(
         finish,

time: 27.7 us -> 27 us (0.975)
  Pallas kernels: 26.9 us -> 26.2 us
    pallas_call x1, Pallas kernels: 25.8 us -> 25.2 us  [on_device(): pl.pallas_call(functools.partial(kernel, sections, tiles), out_shape=(plt...]
where the time goes in v3:
time: 27 us; the launch traced here: 26.8 us
  Pallas kernels  26.2 us (97%)
  between operations  0.64 us (2%)
    pallas_call x1, Pallas kernels, on_device(): pl.pallas_call(functools.partial(kernel, sections, tiles), out_shape=(plt...  25.2 us
    pallas_call x1, Pallas kernels, on_device(): pl.pallas_call(finish, out_shape=(jax.ShapeDtypeStruct(fwd_wave.shape, F3...  1.04 us

profile of v3, /device:TPU:1, one launch (start us, length us, event | category | flops | bytes accessed | tf_op | source)
XLA Modules:
  0.0 26.8 jit_solution(17591505897560922636)
XLA Ops:
  0.6 25.2 %window.1 = (bf16[1,1,2,256,256]{4,3,2,1,0:T(8,128)(2,1)S(1)}, bf16[1,1,2,256,256]{4,3,2,1,0:T(8,128)(2,1)S(1)}, f32[1,256,384]{2,1,0:T(8,128)S(1)}) custom-call(s32[1,2,19]{2,1,0:T(2,128)} %bitcast.1, f32[1,256,384]{2,1,0:T(8,128)} %pot_h.1, bf16[2,256,256]{2,1,0:T(8,128)(2,1)} %probe_h.1, bf16[1,4,256,256]{3,2,1,0:T(8,128)(2,1)} %inten_h.1, ...), custom_call_target="tpu_custom_call" | custom-call | tf_op jit(solution)/shard_map/window/pallas_call | solution.py:497
  25.8 1.0 %finish.1 = (f32[1,1,2,256,256]{4,3,2,1,0:T(8,128)}, bf16[1,1,2,256,256]{4,3,2,1,0:T(8,128)(2,1)}, f32[1,256,384]{2,1,0:T(8,128)}) custom-call(bf16[1,1,2,256,256]{4,3,2,1,0:T(8,128)(2,1)S(1)} %get-tuple-element.6.wave, bf16[1,1,2,256,256]{4,3,2,1,0:T(8,128)(2,1)S(1)} %get-tuple-element.7.adj, f32[1,256,384]{2,1,0:T(8,128)S(1)} %get-tuple-element.8.grad), custom_call_target="tpu_custom_call" | custom-call | tf_op jit(solution)/shard_map/finish/pallas_call | solution.py:525

commit v4 on v3

--- a/solution.py
+++ b/solution.py
@@ -87,9 +87,9 @@
     o_fwd, o_adj, o_grad,
     in_f, in_b, out_f, out_b, main, l_f, r_f, l_g, r_g,
     cs, tf, ta, bk, total, pad, y_buf,
-    halo_out, halo_in, edge_out, edge_in,
+    halo_out, halo_in, edge_out, edge_in, view_out, view_in,
     pos, pot, probe, inten, fwd, adj, saved, ends, load_sem,
-    send_f, recv_f, send_b, recv_b, send_h, recv_h, send_e, recv_e,
+    send_f, recv_f, send_b, recv_b, send_h, recv_h, send_e, recv_e, send_v, recv_v, ready,
 ):
     n = probe.shape[1]
     nc = n // ROWS
@@ -101,6 +101,8 @@
     t = lax.axis_index("tile")
     first, last = s == 0, s == sections - 1
     low, high = t == 0, t == tiles - 1
+    ahead = jnp.logical_and(lax.rem(s, 2) == 0, s > 0)
+    behind = jnp.logical_and(lax.rem(s, 2) == 1, s < sections - 1)
 
     loads = {}
 
@@ -118,7 +120,6 @@
 
     greet(t > 0, "tile", t - 1)
     greet(t < tiles - 1, "tile", t + 1)
-    greet(s > 0, "depth", s - 1)
     greet(s < sections - 1, "depth", s + 1)
     load("pot", pot_h, pot).start()
     load("pos", pos_h, pos).start()
@@ -142,7 +143,7 @@
     loads["pot"].wait()
     halo_out[0] = pot[0, 0:margin, :].astype(BF16)
     halo_out[1] = pot[0, core - margin : core, :].astype(BF16)
-    pl.semaphore_wait(barrier, one(s > 0) + one(s < sections - 1) + one(t > 0) + one(t < tiles - 1))
+    pl.semaphore_wait(barrier, one(s > 0) + one(t > 0) + one(t < tiles - 1))
 
     def hop(src, dst, ssem, rsem, axis, to):
         return pltpu.make_async_remote_copy(
@@ -174,6 +175,10 @@
             down.wait_recv()
 
     tile_start(halo_out, halo_in, send_h, recv_h)
+
+    @pl.when(s > 0)
+    def _():
+        pl.semaphore_signal(ready, inc=1, device_id={"depth": s - 1}, device_id_type=MESH)
 
     def stacked(x):
         return x.reshape(2 * ROWS, n)
@@ -193,6 +198,27 @@
             out = dot(jnp.concatenate([a[0:ROWS, :], a[ROWS : 2 * ROWS, :]], axis=1), r_ref[...])
             sink(o, out[:, 0:n], out[:, n : 2 * n])
 
+    def copy_f(k, c):
+        return hop(out_f.at[k, c], in_f.at[k + 1, c], send_f.at[k, c], recv_f.at[k, c], "depth", s + 1)
+
+    def copy_b(k, c):
+        return hop(out_b.at[k, c], in_b.at[k + 1, c], send_b.at[k, c], recv_b.at[k, c], "depth", s - 1)
+
+    def last_f(c):
+        k, rows = ticks - 1, slice(c * ROWS, (c + 1) * ROWS)
+        return hop(out_f.at[k, c], o_fwd.at[0, 0, :, rows, :], send_f.at[k, c], recv_f.at[k, c], "depth", s + 1)
+
+    def last_b(c):
+        k, rows = ticks - 1, slice(c * ROWS, (c + 1) * ROWS)
+        return hop(out_b.at[k, c], o_adj.at[0, 0, :, rows, :], send_b.at[k, c], recv_b.at[k, c], "depth", s - 1)
+
+    def launch(k, c, copy, final):
+        if isinstance(k, int):
+            copy(k, c).start()
+        else:
+            pl.when(k < ticks - 1)(lambda: copy(k, c).start())
+            pl.when(k == ticks - 1)(lambda: final(c).start())
+
     loads["adj"].wait()
     for c in range(nc):
         rows = slice(c * ROWS, (c + 1) * ROWS)
@@ -204,16 +230,20 @@
         rows = slice(o * ROWS, (o + 1) * ROWS)
         bk[0, rows, :] = lur
         bk[1, rows, :] = lui
+        out_b[0, o, 0] = lur.astype(BF16)
+        out_b[0, o, 1] = lui.astype(BF16)
+        pl.when(ahead)(lambda: copy_b(0, o).start())
 
     product(m_left, lambda c: stacked(in_b[0, c]), main.at[1], keep)
 
     def table(src, dst, count):
         for at in range(0, count, STEP):
-            sv, cv = sin_cos(src(at))
+            v = src(at)
+            sv, cv = sin_cos(v)
             for i in range(cols + 1):
                 one_tile = slice(i * LANES, (i + 1) * LANES)
-                cs[i, pl.ds(2 * (dst + at), STEP, stride=2), :] = cv[:, one_tile]
-                cs[i, pl.ds(2 * (dst + at) + 1, STEP, stride=2), :] = sv[:, one_tile]
+                for part, part_v in enumerate((cv, sv, v)):
+                    cs[i, pl.ds(3 * (dst + at) + part, STEP, stride=3), :] = part_v[:, one_tile]
 
     table(lambda at: pot[0, at : at + STEP, :], margin, core)
     total[...] = jnp.zeros_like(total)
@@ -279,20 +309,40 @@
 
     lane = lax.broadcasted_iota(jnp.int32, (STEP, LANES), 1)
 
-    def window(index, out, slot):
+    def window(index, parts, store):
         r, c = pos[0, 0, index], pos[0, 1, index]
         turn = lax.rem(LANES - c, LANES)
         own = lane < LANES - c
-        for part in range(2):
+        for part in parts:
             for at in range(0, n, STEP):
-                rows = pl.ds(2 * (r + at) + part, STEP, stride=2)
+                rows = pl.ds(3 * (r + at) + part, STEP, stride=3)
                 x = [pltpu.roll(cs[i, rows, :], turn, 1) for i in range(cols + 1)]
                 for i in range(cols):
-                    out[slot, part, at : at + STEP, i * LANES : (i + 1) * LANES] = jnp.where(own, x[i], x[i + 1])
+                    store(part, at, slice(i * LANES, (i + 1) * LANES), jnp.where(own, x[i], x[i + 1]))
+
+    def window_b(k):
+        def store(part, at, tile, x):
+            ta[lax.rem(k, 2), part, at : at + STEP, tile] = x
+        window(k + s, range(2), store)
+
+    def window_f(k):
+        def store(part, at, tile, x):
+            tf[lax.rem(k, 2), part, at : at + STEP, tile] = x
+        window(k - s + 2 * sections - 1, range(2), store)
+
+    def copy_v(c):
+        return hop(view_out.at[c], view_in.at[c], send_v.at[c], recv_v.at[c], "depth", s - 1)
+
+    def send_view():
+        def store(part, at, tile, x):
+            view_out[at // ROWS, at % ROWS : at % ROWS + STEP, tile] = x.astype(BF16)
+        window(s, (2,), store)
+        for c in range(nc):
+            copy_v(c).start()
 
     def windows(k):
-        window(k + s, ta, lax.rem(k, 2))
-        window(k - s + 2 * sections - 1, tf, lax.rem(k, 2))
+        window_b(k)
+        window_f(k)
 
     def scatter(k):
         r, c = pos[0, 0, k + s], pos[0, 1, k + s]
@@ -308,15 +358,23 @@
             d = [zero] + d + [zero]
             for i in range(cols + 1):
                 pad[i, pl.ds(2 * (spare + at), STEP, stride=2), :] = jnp.where(own, d[i + 1], d[i])
-        for at in range(0, width, STEP):
-            for i in range(cols + 1):
-                total[at : at + STEP, i * LANES : (i + 1) * LANES] += pad[i, pl.ds(2 * (spare - r + at), STEP, stride=2), :]
-
-    def copy_f(k, c):
-        return hop(out_f.at[k, c], in_f.at[k + 1, c], send_f.at[k, c], recv_f.at[k, c], "depth", s + 1)
-
-    def copy_b(k, c):
-        return hop(out_b.at[k, c], in_b.at[k + 1, c], send_b.at[k, c], recv_b.at[k, c], "depth", s - 1)
+
+        def add(lo, hi):
+            for at in range(lo, hi, STEP):
+                for i in range(cols + 1):
+                    total[at : at + STEP, i * LANES : (i + 1) * LANES] += pad[
+                        i, pl.ds(2 * (spare - r + at), STEP, stride=2), :
+                    ]
+
+        add(0, margin)
+        add(margin + core, width)
+        if not isinstance(k, int):
+            @pl.when(k == ticks - 1)
+            def _():
+                edge_out[0] = total[0:margin, :].astype(BF16)
+                edge_out[1] = total[margin + core :, :].astype(BF16)
+                tile_start(edge_out, edge_in, send_e, recv_e)
+        add(margin, margin + core)
 
     def send_back(k, c, lur, lui):
         rows = slice(c * ROWS, (c + 1) * ROWS)
@@ -326,18 +384,30 @@
         bi = tr * lui + ti * lur
         bk[0, rows, :] = br
         bk[1, rows, :] = bi
-        out_b[k, c, 0] = br.astype(BF16)
-        out_b[k, c, 1] = bi.astype(BF16)
-
-        @pl.when(jnp.logical_not(first))
+
+        sends = jnp.logical_not(first)
+        if isinstance(k, int):
+            sends = jnp.logical_and(sends, jnp.logical_not(ahead))
+
+        @pl.when(sends)
         def _():
-            copy_b(k, c).start()
-
-    def backward(k):
+            out_b[k, c, 0] = br.astype(BF16)
+            out_b[k, c, 1] = bi.astype(BF16)
+            launch(k, c, copy_b, last_b)
+
+    def backward(k, bare=False):
         def arrived(c):
             @pl.when(jnp.logical_not(last))
             def _():
                 copy_b(k - 1, c).wait_recv()
+            if bare:
+                @pl.when(jnp.logical_and(k == 1, behind))
+                def _():
+                    copy_v(c).wait_recv()
+                    lur, lui = in_b[1, c, 0].astype(F32), in_b[1, c, 1].astype(F32)
+                    ti, tr = sin_cos(view_in[c].astype(F32))
+                    in_b[1, c, 0] = (tr * lur - ti * lui).astype(BF16)
+                    in_b[1, c, 1] = (tr * lui + ti * lur).astype(BF16)
             return stacked(in_b[k, c])
 
         product(m_left, arrived, main.at[1], functools.partial(send_back, k))
@@ -357,7 +427,7 @@
         def sink(c, outr, outi):
             out_f[k, c, 0] = outr.astype(BF16)
             out_f[k, c, 1] = outi.astype(BF16)
-            copy_f(k, c).start()
+            launch(k, c, copy_f, last_f)
 
         product(m_left, lambda c: entering(k, c, waits), main.at[1], sink)
 
@@ -376,13 +446,16 @@
         product(lambda o, c: l_g[o, c], lambda c: y_buf[c], r_g, seed)
 
     loads["pos"].wait()
-    windows(0)
+    pl.when(ahead)(send_view)
+    window_b(0)
     for c in range(nc):
         rows = slice(c * ROWS, (c + 1) * ROWS)
         send_back(0, c, bk[0, rows, :], bk[1, rows, :])
+    window_f(0)
 
     @pl.when(jnp.logical_not(last))
     def _():
+        pl.semaphore_wait(ready, 1)
         forward(0, False)
 
     @pl.when(last)
@@ -403,7 +476,7 @@
             @pl.when(k < ticks - 1)
             def _():
                 windows(k + 1)
-            backward(k)
+            backward(k, True)
             scatter(k)
             return carry
         lax.fori_loop(1, ticks, tick, 0)
@@ -428,25 +501,25 @@
             return carry
         lax.fori_loop(1, ticks, tick, 0)
 
-    edge_out[0] = total[0:margin, :].astype(BF16)
-    edge_out[1] = total[margin + core :, :].astype(BF16)
-    tile_start(edge_out, edge_in, send_e, recv_e)
     o_grad[0, margin : core - margin, :] = total[2 * margin : core, :]
     tile_wait(edge_out, edge_in, send_e, recv_e)
     o_grad[0, 0:margin, :] = total[margin : 2 * margin, :] + edge_in[0].astype(F32)
     o_grad[0, core - margin : core, :] = total[core : core + margin, :] + edge_in[1].astype(F32)
+    @pl.when(last)
+    def _():
+        for c in range(nc):
+            o_adj[0, 0, :, c * ROWS : (c + 1) * ROWS, :] = in_b[ticks, c]
+
     for c in range(nc):
-        rows = slice(c * ROWS, (c + 1) * ROWS)
-
         @pl.when(jnp.logical_not(last))
         def _():
-            copy_b(ticks - 1, c).wait_recv()
-        o_adj[0, 0, :, rows, :] = in_b[ticks, c]
+            last_b(c).wait_recv()
 
         @pl.when(jnp.logical_not(first))
         def _():
-            copy_f(ticks - 1, c).wait_recv()
-            o_fwd[0, 0, :, rows, :] = in_f[ticks, c]
+            last_f(c).wait_recv()
+    for c in range(nc):
+        pl.when(ahead)(lambda: copy_v(c).wait_send())
     for k in range(ticks):
         for c in range(nc):
             @pl.when(jnp.logical_not(last))
@@ -506,14 +579,14 @@
         scratch_shapes=[
             wave(ticks + 1), wave(ticks + 1), wave(ticks), wave(ticks),
             held(main), lt, rt, lt, rt,
-            pltpu.VMEM((width // LANES, 2 * width, LANES), F32), pair, pair, pltpu.VMEM((2, n, n), F32),
+            pltpu.VMEM((width // LANES, 3 * width, LANES), F32), pair, pair, pltpu.VMEM((2, n, n), F32),
             square, pltpu.VMEM((width // LANES, 4 * width - 2 * n, LANES), F32),
             pltpu.VMEM((nc, 2 * ROWS, n), BF16),
-            strip, strip, strip, strip,
+            strip, strip, strip, strip, pltpu.VMEM((nc, ROWS, n), BF16), pltpu.VMEM((nc, ROWS, n), BF16),
             pltpu.SMEM(spots.shape, spots.dtype), held(potential), held(probe), held(intensity), held(fwd_wave), held(adj_wave),
             held(saved_wave), held(ends), dma(9),
             dma(ticks, nc), dma(ticks, nc), dma(ticks, nc), dma(ticks, nc),
-            dma(2), dma(2), dma(2), dma(2),
+            dma(2), dma(2), dma(2), dma(2), dma(nc), dma(nc), pltpu.SemaphoreType.REGULAR,
         ],
         compiler_params=pltpu.CompilerParams(
             collective_id=0, has_side_effects=True, vmem_limit_bytes=VLIM * 1024 * 1024

time: 27 us -> 25.2 us (0.933)
  Pallas kernels: 26.2 us -> 24.4 us
    pallas_call x1, Pallas kernels: 25.2 us -> 23.3 us  [on_device(): pl.pallas_call(functools.partial(kernel, sections, tiles), out_shape=(plt...]
where the time goes in v4:
time: 25.2 us; the launch traced here: 25 us
  Pallas kernels  24.4 us (97%)
  between operations  0.64 us (3%)
    pallas_call x1, Pallas kernels, on_device(): pl.pallas_call(functools.partial(kernel, sections, tiles), out_shape=(plt...  23.3 us
    pallas_call x1, Pallas kernels, on_device(): pl.pallas_call(finish, out_shape=(jax.ShapeDtypeStruct(fwd_wave.shape, F3...  1.04 us

profile of v4, /device:TPU:1, one launch (start us, length us, event | category | flops | bytes accessed | tf_op | source)
XLA Modules:
  0.0 25.0 jit_solution(4167299252442644452)
XLA Ops:
  0.6 23.3 %window.1 = (bf16[1,1,2,256,256]{4,3,2,1,0:T(8,128)(2,1)S(1)}, bf16[1,1,2,256,256]{4,3,2,1,0:T(8,128)(2,1)S(1)}, f32[1,256,384]{2,1,0:T(8,128)S(1)}) custom-call(s32[1,2,19]{2,1,0:T(2,128)} %bitcast.1, f32[1,256,384]{2,1,0:T(8,128)} %pot_h.1, bf16[2,256,256]{2,1,0:T(8,128)(2,1)} %probe_h.1, bf16[1,4,256,256]{3,2,1,0:T(8,128)(2,1)} %inten_h.1, ...), custom_call_target="tpu_custom_call" | custom-call | tf_op jit(solution)/shard_map/window/pallas_call | solution.py:570
  24.0 1.0 %finish.1 = (f32[1,1,2,256,256]{4,3,2,1,0:T(8,128)}, bf16[1,1,2,256,256]{4,3,2,1,0:T(8,128)(2,1)}, f32[1,256,384]{2,1,0:T(8,128)}) custom-call(bf16[1,1,2,256,256]{4,3,2,1,0:T(8,128)(2,1)S(1)} %get-tuple-element.6.wave, bf16[1,1,2,256,256]{4,3,2,1,0:T(8,128)(2,1)S(1)} %get-tuple-element.7.adj, f32[1,256,384]{2,1,0:T(8,128)S(1)} %get-tuple-element.8.grad), custom_call_target="tpu_custom_call" | custom-call | tf_op jit(solution)/shard_map/finish/pallas_call | solution.py:598

commit v5 on v4

--- a/solution.py
+++ b/solution.py
@@ -85,11 +85,11 @@
     sections, tiles,
     pos_h, pot_h, probe_h, inten_h, fwd_h, adj_h, saved_h, main_h, ends_h,
     o_fwd, o_adj, o_grad,
-    in_f, in_b, out_f, out_b, main, l_f, r_f, l_g, r_g,
-    cs, tf, ta, bk, total, pad, y_buf,
-    halo_out, halo_in, edge_out, edge_in, view_out, view_in,
+    in_f, in_b, out_f, out_b, out_r, main, l_f, r_f, l_g, r_g,
+    cs, tf, ta, tv, bk, total, pad, y_buf,
+    halo_out, halo_in, edge_out, edge_in, view_out, view_in, side_out, side_in,
     pos, pot, probe, inten, fwd, adj, saved, ends, load_sem,
-    send_f, recv_f, send_b, recv_b, send_h, recv_h, send_e, recv_e, send_v, recv_v, ready,
+    send_f, recv_f, send_b, recv_b, send_h, recv_h, send_e, recv_e, send_v, recv_v, send_r, send_s, recv_s, ready,
 ):
     n = probe.shape[1]
     nc = n // ROWS
@@ -101,6 +101,9 @@
     t = lax.axis_index("tile")
     first, last = s == 0, s == sections - 1
     low, high = t == 0, t == tiles - 1
+    odd = lax.rem(s, 2) == 1
+    relay = jnp.logical_and(odd, s > 1)
+    aside = jnp.logical_and(jnp.logical_not(odd), jnp.logical_and(s > 0, s < sections - 1))
     ahead = jnp.logical_and(lax.rem(s, 2) == 0, s > 0)
     behind = jnp.logical_and(lax.rem(s, 2) == 1, s < sections - 1)
 
@@ -121,6 +124,7 @@
     greet(t > 0, "tile", t - 1)
     greet(t < tiles - 1, "tile", t + 1)
     greet(s < sections - 1, "depth", s + 1)
+    greet(jnp.logical_and(odd, s < sections - 2), "depth", s + 2)
     load("pot", pot_h, pot).start()
     load("pos", pos_h, pos).start()
     load("main", main_h, main).start()
@@ -143,7 +147,7 @@
     loads["pot"].wait()
     halo_out[0] = pot[0, 0:margin, :].astype(BF16)
     halo_out[1] = pot[0, core - margin : core, :].astype(BF16)
-    pl.semaphore_wait(barrier, one(s > 0) + one(t > 0) + one(t < tiles - 1))
+    pl.semaphore_wait(barrier, one(s > 0) + one(relay) + one(t > 0) + one(t < tiles - 1))
 
     def hop(src, dst, ssem, rsem, axis, to):
         return pltpu.make_async_remote_copy(
@@ -204,20 +208,19 @@
     def copy_b(k, c):
         return hop(out_b.at[k, c], in_b.at[k + 1, c], send_b.at[k, c], recv_b.at[k, c], "depth", s - 1)
 
-    def last_f(c):
-        k, rows = ticks - 1, slice(c * ROWS, (c + 1) * ROWS)
-        return hop(out_f.at[k, c], o_fwd.at[0, 0, :, rows, :], send_f.at[k, c], recv_f.at[k, c], "depth", s + 1)
+    def copy_r(k, c):
+        return hop(out_r.at[k, c], in_b.at[k + 2, c], send_r.at[k, c], recv_b.at[k + 1, c], "depth", s - 2)
+
+    def last_r(c):
+        k, rows = ticks - 2, slice(c * ROWS, (c + 1) * ROWS)
+        return hop(out_r.at[k, c], o_adj.at[0, 0, :, rows, :], send_r.at[k, c], recv_b.at[k + 1, c], "depth", s - 2)
+
+    def copy_s(k, c):
+        return hop(side_out.at[k, c], side_in.at[k, c], send_s.at[k, c], recv_s.at[k, c], "depth", s + 1)
 
     def last_b(c):
         k, rows = ticks - 1, slice(c * ROWS, (c + 1) * ROWS)
         return hop(out_b.at[k, c], o_adj.at[0, 0, :, rows, :], send_b.at[k, c], recv_b.at[k, c], "depth", s - 1)
-
-    def launch(k, c, copy, final):
-        if isinstance(k, int):
-            copy(k, c).start()
-        else:
-            pl.when(k < ticks - 1)(lambda: copy(k, c).start())
-            pl.when(k == ticks - 1)(lambda: final(c).start())
 
     loads["adj"].wait()
     for c in range(nc):
@@ -236,16 +239,18 @@
 
     product(m_left, lambda c: stacked(in_b[0, c]), main.at[1], keep)
 
-    def table(src, dst, count):
-        for at in range(0, count, STEP):
-            v = src(at)
-            sv, cv = sin_cos(v)
-            for i in range(cols + 1):
-                one_tile = slice(i * LANES, (i + 1) * LANES)
-                for part, part_v in enumerate((cv, sv, v)):
-                    cs[i, pl.ds(3 * (dst + at) + part, STEP, stride=3), :] = part_v[:, one_tile]
-
-    table(lambda at: pot[0, at : at + STEP, :], margin, core)
+    def place(part, at, x):
+        for i in range(cols + 1):
+            cs[i, pl.ds(3 * at + part, STEP, stride=3), :] = x[:, i * LANES : (i + 1) * LANES]
+
+    def phase_table(at, v):
+        sv, cv = sin_cos(v)
+        place(0, at, cv)
+        place(1, at, sv)
+
+    for at in range(0, core, STEP):
+        place(2, margin + at, pot[0, at : at + STEP, :])
+        phase_table(margin + at, pot[0, at : at + STEP, :])
     total[...] = jnp.zeros_like(total)
     spare = width - n
     for i in range(cols + 1):
@@ -260,12 +265,10 @@
     @pl.when(first)
     def _():
         loads["probe"].wait()
-        for k in range(ticks - 1):
+        for k in range(ticks):
             for c in range(nc):
                 for part in range(2):
                     in_f[k + 1, c, part] = probe[part, c * ROWS : (c + 1) * ROWS, :]
-        for part in range(2):
-            o_fwd[0, 0, part] = probe[part]
 
     @pl.when(last)
     def _():
@@ -303,18 +306,20 @@
         halo_in[1] = jnp.zeros((margin, width), BF16)
         edge_in[1] = jnp.zeros((margin, width), BF16)
 
+    loads["pos"].wait()
     tile_wait(halo_out, halo_in, send_h, recv_h)
-    table(lambda at: halo_in[0, at : at + STEP, :].astype(F32), 0, margin)
-    table(lambda at: halo_in[1, at : at + STEP, :].astype(F32), margin + core, margin)
+    strips = [(side * (margin + core) + at, side, slice(at, at + STEP)) for side in range(2) for at in range(0, margin, STEP)]
+    for at, side, rows in strips:
+        place(2, at, halo_in[side, rows, :].astype(F32))
 
     lane = lax.broadcasted_iota(jnp.int32, (STEP, LANES), 1)
 
-    def window(index, parts, store):
+    def window(index, parts, store, steps=range(0, n, STEP)):
         r, c = pos[0, 0, index], pos[0, 1, index]
         turn = lax.rem(LANES - c, LANES)
         own = lane < LANES - c
         for part in parts:
-            for at in range(0, n, STEP):
+            for at in steps:
                 rows = pl.ds(3 * (r + at) + part, STEP, stride=3)
                 x = [pltpu.roll(cs[i, rows, :], turn, 1) for i in range(cols + 1)]
                 for i in range(cols):
@@ -333,12 +338,24 @@
     def copy_v(c):
         return hop(view_out.at[c], view_in.at[c], send_v.at[c], recv_v.at[c], "depth", s - 1)
 
-    def send_view():
+    def send_views(index, out, copy):
         def store(part, at, tile, x):
-            view_out[at // ROWS, at % ROWS : at % ROWS + STEP, tile] = x.astype(BF16)
-        window(s, (2,), store)
+            out[at // ROWS, at % ROWS : at % ROWS + STEP, tile] = x.astype(BF16)
         for c in range(nc):
-            copy_v(c).start()
+            window(index, (2,), store, range(c * ROWS, (c + 1) * ROWS, STEP))
+            copy(c).start()
+
+    def send_aside(k):
+        send_views(k + s + 1, side_out.at[k], functools.partial(copy_s, k))
+
+    def side_phase(k):
+        for c in range(nc):
+            copy_s(k, c).wait_recv()
+            for at in range(0, ROWS, STEP):
+                sv, cv = sin_cos(side_in[k, c, at : at + STEP, :].astype(F32))
+                rows = slice(c * ROWS + at, c * ROWS + at + STEP)
+                tv[lax.rem(k, 2), 0, rows, :] = cv
+                tv[lax.rem(k, 2), 1, rows, :] = sv
 
     def windows(k):
         window_b(k)
@@ -348,16 +365,17 @@
         r, c = pos[0, 0, k + s], pos[0, 1, k + s]
         own = lane >= c
         turn = lax.rem(c, LANES)
-        for at in range(0, n, STEP):
-            rows = slice(at, at + STEP)
-            sr = saved[0, 0, k, 0, rows, :].astype(F32)
-            si = saved[0, 0, k, 1, rows, :].astype(F32)
-            d = (bk[1, rows, :] * sr + bk[0, rows, :] * si) * -SIGMA
-            d = [pltpu.roll(d[:, i * LANES : (i + 1) * LANES], turn, 1) for i in range(cols)]
-            zero = jnp.zeros((STEP, LANES), F32)
-            d = [zero] + d + [zero]
-            for i in range(cols + 1):
-                pad[i, pl.ds(2 * (spare + at), STEP, stride=2), :] = jnp.where(own, d[i + 1], d[i])
+        def lay(lo, hi):
+            for at in range(lo, hi, STEP):
+                rows = slice(at, at + STEP)
+                sr = saved[0, 0, k, 0, rows, :].astype(F32)
+                si = saved[0, 0, k, 1, rows, :].astype(F32)
+                d = (bk[1, rows, :] * sr + bk[0, rows, :] * si) * -SIGMA
+                d = [pltpu.roll(d[:, i * LANES : (i + 1) * LANES], turn, 1) for i in range(cols)]
+                zero = jnp.zeros((STEP, LANES), F32)
+                d = [zero] + d + [zero]
+                for i in range(cols + 1):
+                    pad[i, pl.ds(2 * (spare + at), STEP, stride=2), :] = jnp.where(own, d[i + 1], d[i])
 
         def add(lo, hi):
             for at in range(lo, hi, STEP):
@@ -366,6 +384,8 @@
                         i, pl.ds(2 * (spare - r + at), STEP, stride=2), :
                     ]
 
+        lay(0, margin)
+        lay(n - margin, n)
         add(0, margin)
         add(margin + core, width)
         if not isinstance(k, int):
@@ -374,6 +394,7 @@
                 edge_out[0] = total[0:margin, :].astype(BF16)
                 edge_out[1] = total[margin + core :, :].astype(BF16)
                 tile_start(edge_out, edge_in, send_e, recv_e)
+        lay(margin, n - margin)
         add(margin, margin + core)
 
     def send_back(k, c, lur, lui):
@@ -385,32 +406,54 @@
         bk[0, rows, :] = br
         bk[1, rows, :] = bi
 
-        sends = jnp.logical_not(first)
         if isinstance(k, int):
-            sends = jnp.logical_and(sends, jnp.logical_not(ahead))
-
-        @pl.when(sends)
+            @pl.when(odd)
+            def _():
+                out_b[k, c, 0] = br.astype(BF16)
+                out_b[k, c, 1] = bi.astype(BF16)
+                copy_b(k, c).start()
+            return
+
+        @pl.when(odd)
         def _():
             out_b[k, c, 0] = br.astype(BF16)
-            out_b[k, c, 1] = bi.astype(BF16)
-            launch(k, c, copy_b, last_b)
-
-    def backward(k, bare=False):
+            out_b[k, c, 1] = (bi * jnp.where(k == ticks - 1, -1.0, 1.0)).astype(BF16)
+            pl.when(k < ticks - 1)(lambda: copy_b(k, c).start())
+            pl.when(k == ticks - 1)(lambda: last_b(c).start())
+
+    def backward(k):
         def arrived(c):
             @pl.when(jnp.logical_not(last))
             def _():
                 copy_b(k - 1, c).wait_recv()
-            if bare:
-                @pl.when(jnp.logical_and(k == 1, behind))
-                def _():
-                    copy_v(c).wait_recv()
-                    lur, lui = in_b[1, c, 0].astype(F32), in_b[1, c, 1].astype(F32)
-                    ti, tr = sin_cos(view_in[c].astype(F32))
-                    in_b[1, c, 0] = (tr * lur - ti * lui).astype(BF16)
-                    in_b[1, c, 1] = (tr * lui + ti * lur).astype(BF16)
+
+            @pl.when(jnp.logical_and(k == 1, behind))
+            def _():
+                copy_v(c).wait_recv()
+                lur, lui = in_b[1, c, 0].astype(F32), in_b[1, c, 1].astype(F32)
+                ti, tr = sin_cos(view_in[c].astype(F32))
+                in_b[1, c, 0] = (tr * lur - ti * lui).astype(BF16)
+                in_b[1, c, 1] = (tr * lui + ti * lur).astype(BF16)
             return stacked(in_b[k, c])
 
         product(m_left, arrived, main.at[1], functools.partial(send_back, k))
+
+    def pass_on(k):
+        def sink(c, lur, lui):
+            rows = slice(c * ROWS, (c + 1) * ROWS)
+            slot = lax.rem(k, 2)
+            tr, ti = tv[slot, 0, rows, :], tv[slot, 1, rows, :]
+            out_r[k, c, 0] = (tr * lur - ti * lui).astype(BF16)
+            bi = tr * lui + ti * lur
+            if isinstance(k, int):
+                out_r[k, c, 1] = bi.astype(BF16)
+                copy_r(k, c).start()
+            else:
+                out_r[k, c, 1] = (bi * jnp.where(k == ticks - 2, -1.0, 1.0)).astype(BF16)
+                pl.when(k < ticks - 2)(lambda: copy_r(k, c).start())
+                pl.when(k == ticks - 2)(lambda: last_r(c).start())
+
+        product(m_left, lambda c: stacked(out_b[k, c]), main.at[1], sink)
 
     def entering(k, c, waits):
         if waits:
@@ -427,7 +470,7 @@
         def sink(c, outr, outi):
             out_f[k, c, 0] = outr.astype(BF16)
             out_f[k, c, 1] = outi.astype(BF16)
-            launch(k, c, copy_f, last_f)
+            copy_f(k, c).start()
 
         product(m_left, lambda c: entering(k, c, waits), main.at[1], sink)
 
@@ -445,8 +488,17 @@
         product(lambda o, c: l_f[o, c], lambda c: entering(k, c, waits), r_f, detect)
         product(lambda o, c: l_g[o, c], lambda c: y_buf[c], r_g, seed)
 
-    loads["pos"].wait()
-    pl.when(ahead)(send_view)
+    @pl.when(ahead)
+    def _():
+        send_views(s, view_out, copy_v)
+
+    @pl.when(jnp.logical_not(last))
+    def _():
+        pl.semaphore_wait(ready, 1)
+
+    pl.when(aside)(lambda: send_aside(0))
+    for at, side, rows in strips:
+        phase_table(at, halo_in[side, rows, :].astype(F32))
     window_b(0)
     for c in range(nc):
         rows = slice(c * ROWS, (c + 1) * ROWS)
@@ -455,14 +507,24 @@
 
     @pl.when(jnp.logical_not(last))
     def _():
-        pl.semaphore_wait(ready, 1)
         forward(0, False)
 
     @pl.when(last)
     def _():
         forward_last(0, False)
 
+    @pl.when(relay)
+    def _():
+        side_phase(0)
+        pass_on(0)
+
+    @pl.when(aside)
+    def _():
+        for k in range(1, ticks - 1):
+            send_aside(k)
+
     windows(1)
+    pl.when(relay)(lambda: side_phase(1))
     loads["saved"].wait()
     scatter(0)
 
@@ -476,7 +538,9 @@
             @pl.when(k < ticks - 1)
             def _():
                 windows(k + 1)
-            backward(k, True)
+            pl.when(jnp.logical_and(relay, k < ticks - 2))(lambda: side_phase(k + 1))
+            backward(k)
+            pl.when(jnp.logical_and(relay, k < ticks - 1))(lambda: pass_on(k))
             scatter(k)
             return carry
         lax.fori_loop(1, ticks, tick, 0)
@@ -485,11 +549,13 @@
     def _():
         def tick(k, carry):
             backward(k)
+            pl.when(jnp.logical_and(relay, k < ticks - 1))(lambda: pass_on(k))
             scatter(k)
 
             @pl.when(k < ticks - 1)
             def _():
                 windows(k + 1)
+            pl.when(jnp.logical_and(relay, k < ticks - 2))(lambda: side_phase(k + 1))
 
             @pl.when(jnp.logical_not(last))
             def _():
@@ -502,47 +568,48 @@
         lax.fori_loop(1, ticks, tick, 0)
 
     o_grad[0, margin : core - margin, :] = total[2 * margin : core, :]
+    for c in range(nc):
+        @pl.when(jnp.logical_not(first))
+        def _():
+            copy_f(ticks - 1, c).wait_recv()
+        o_fwd[0, 0, :, c * ROWS : (c + 1) * ROWS, :] = in_f[ticks, c].astype(F32)
     tile_wait(edge_out, edge_in, send_e, recv_e)
     o_grad[0, 0:margin, :] = total[margin : 2 * margin, :] + edge_in[0].astype(F32)
     o_grad[0, core - margin : core, :] = total[core : core + margin, :] + edge_in[1].astype(F32)
+
     @pl.when(last)
     def _():
         for c in range(nc):
-            o_adj[0, 0, :, c * ROWS : (c + 1) * ROWS, :] = in_b[ticks, c]
+            rows = slice(c * ROWS, (c + 1) * ROWS)
+            o_adj[0, 0, 0, rows, :] = in_b[ticks, c, 0]
+            o_adj[0, 0, 1, rows, :] = -in_b[ticks, c, 1]
+
+    @pl.when(jnp.logical_not(last))
+    def _():
+        for c in range(nc):
+            last_b(c).wait_recv()
 
     for c in range(nc):
-        @pl.when(jnp.logical_not(last))
+        @pl.when(ahead)
         def _():
-            last_b(c).wait_recv()
-
-        @pl.when(jnp.logical_not(first))
-        def _():
-            last_f(c).wait_recv()
-    for c in range(nc):
-        pl.when(ahead)(lambda: copy_v(c).wait_send())
-    for k in range(ticks):
-        for c in range(nc):
-            @pl.when(jnp.logical_not(last))
-            def _():
-                copy_f(k, c).wait_send()
-
-            @pl.when(jnp.logical_not(first))
-            def _():
-                copy_b(k, c).wait_send()
-
-
-def finish(wave, adj, grad, o_wave, o_adj, o_grad, wave_buf, adj_buf, sem):
-    moves = [pltpu.make_async_copy(grad, o_grad, sem.at[0])]
-    moves[0].start()
-    for part in range(2):
-        wave_buf[0, 0, part] = wave[0, 0, part].astype(F32)
-        move = pltpu.make_async_copy(wave_buf.at[0, 0, part], o_wave.at[0, 0, part], sem.at[1 + part])
+            copy_v(c).wait_send()
+            copy_b(0, c).wait_send()
+
+        for k in range(ticks):
+            pl.when(jnp.logical_not(last))(lambda: copy_f(k, c).wait_send())
+            pl.when(odd)(lambda: copy_b(k, c).wait_send())
+        for k in range(ticks - 1):
+            pl.when(relay)(lambda: copy_r(k, c).wait_send())
+            pl.when(aside)(lambda: copy_s(k, c).wait_send())
+
+
+def finish(wave, adj, grad, o_wave, o_adj, o_grad, sem):
+    moves = [
+        pltpu.make_async_copy(src, dst, sem.at[i])
+        for i, (src, dst) in enumerate(((wave, o_wave), (grad, o_grad), (adj, o_adj)))
+    ]
+    for move in moves:
         move.start()
-        moves.append(move)
-    adj_buf[0, 0, 0] = adj[0, 0, 0]
-    adj_buf[0, 0, 1] = -adj[0, 0, 1]
-    moves.append(pltpu.make_async_copy(adj_buf, o_adj, sem.at[3]))
-    moves[-1].start()
     for move in moves:
         move.wait()
 
@@ -566,27 +633,30 @@
     rt = pltpu.VMEM((2 * n, 2 * n), BF16)
     square = pltpu.VMEM((width, width), F32)
     pair = pltpu.VMEM((2, 2, n, n), F32)
+    view = lambda *count: pltpu.VMEM((*count, ROWS, n), BF16)
     strip = pltpu.VMEM((2, margin, width), BF16)
     wave_next, adj_next, gradient = pl.pallas_call(
         functools.partial(kernel, sections, tiles),
         out_shape=(
-            pltpu.VMEM(fwd_wave.shape, BF16),
+            pltpu.VMEM(fwd_wave.shape, F32),
             pltpu.VMEM(adj_wave.shape, BF16),
             pltpu.VMEM(potential.shape, F32),
         ),
         in_specs=[hbm] * 9,
         out_specs=(vmem, vmem, vmem),
         scratch_shapes=[
-            wave(ticks + 1), wave(ticks + 1), wave(ticks), wave(ticks),
+            wave(ticks + 1), wave(ticks + 1), wave(ticks), wave(ticks), wave(ticks - 1),
             held(main), lt, rt, lt, rt,
-            pltpu.VMEM((width // LANES, 3 * width, LANES), F32), pair, pair, pltpu.VMEM((2, n, n), F32),
+            pltpu.VMEM((width // LANES, 3 * width, LANES), F32), pair, pair, pair, pltpu.VMEM((2, n, n), F32),
             square, pltpu.VMEM((width // LANES, 4 * width - 2 * n, LANES), F32),
             pltpu.VMEM((nc, 2 * ROWS, n), BF16),
-            strip, strip, strip, strip, pltpu.VMEM((nc, ROWS, n), BF16), pltpu.VMEM((nc, ROWS, n), BF16),
+            strip, strip, strip, strip, view(nc), view(nc),
+            view(ticks - 1, nc), view(ticks - 1, nc),
             pltpu.SMEM(spots.shape, spots.dtype), held(potential), held(probe), held(intensity), held(fwd_wave), held(adj_wave),
             held(saved_wave), held(ends), dma(9),
             dma(ticks, nc), dma(ticks, nc), dma(ticks, nc), dma(ticks, nc),
-            dma(2), dma(2), dma(2), dma(2), dma(nc), dma(nc), pltpu.SemaphoreType.REGULAR,
+            dma(2), dma(2), dma(2), dma(2), dma(nc), dma(nc),
+            dma(ticks - 1, nc), dma(ticks - 1, nc), dma(ticks - 1, nc), pltpu.SemaphoreType.REGULAR,
         ],
         compiler_params=pltpu.CompilerParams(
             collective_id=0, has_side_effects=True, vmem_limit_bytes=VLIM * 1024 * 1024
@@ -604,7 +674,7 @@
         ),
         in_specs=[vmem, vmem, vmem],
         out_specs=(hbm, hbm, hbm),
-        scratch_shapes=[pltpu.VMEM(fwd_wave.shape, F32), held(adj_wave), dma(4)],
+        scratch_shapes=[dma(3)],
         name="finish",
     )(near(wave_next), near(adj_next), near(gradient))
 

time: 25.2 us -> 24.3 us (0.964)
  Pallas kernels: 24.4 us -> 23.5 us
    pallas_call x1, Pallas kernels: 23.3 us -> 22.5 us  [on_device(): pl.pallas_call(functools.partial(kernel, sections, tiles), out_shape=(plt...]
where the time goes in v5:
time: 24.3 us; the launch traced here: 24.1 us
  Pallas kernels  23.5 us (97%)
  between operations  0.64 us (3%)
    pallas_call x1, Pallas kernels, on_device(): pl.pallas_call(functools.partial(kernel, sections, tiles), out_shape=(plt...  22.5 us
    pallas_call x1, Pallas kernels, on_device(): pl.pallas_call(finish, out_shape=(jax.ShapeDtypeStruct(fwd_wave.shape, F3...  1.03 us

profile of v5, /device:TPU:1, one launch (start us, length us, event | category | flops | bytes accessed | tf_op | source)
XLA Modules:
  0.0 24.1 jit_solution(17728938579842838527)
XLA Ops:
  0.6 22.5 %window.1 = (f32[1,1,2,256,256]{4,3,2,1,0:T(8,128)S(1)}, bf16[1,1,2,256,256]{4,3,2,1,0:T(8,128)(2,1)S(1)}, f32[1,256,384]{2,1,0:T(8,128)S(1)}) custom-call(s32[1,2,19]{2,1,0:T(2,128)} %bitcast.1, f32[1,256,384]{2,1,0:T(8,128)} %pot_h.1, bf16[2,256,256]{2,1,0:T(8,128)(2,1)} %probe_h.1, bf16[1,4,256,256]{3,2,1,0:T(8,128)(2,1)} %inten_h.1, ...), custom_call_target="tpu_custom_call" | custom-call | tf_op jit(solution)/shard_map/window/pallas_call | solution.py:638
  23.1 1.0 %finish.1 = (f32[1,1,2,256,256]{4,3,2,1,0:T(8,128)}, bf16[1,1,2,256,256]{4,3,2,1,0:T(8,128)(2,1)}, f32[1,256,384]{2,1,0:T(8,128)}) custom-call(f32[1,1,2,256,256]{4,3,2,1,0:T(8,128)S(1)} %get-tuple-element.6.wave, bf16[1,1,2,256,256]{4,3,2,1,0:T(8,128)(2,1)S(1)} %get-tuple-element.7.adj, f32[1,256,384]{2,1,0:T(8,128)S(1)} %get-tuple-element.8.grad), custom_call_target="tpu_custom_call" | custom-call | tf_op jit(solution)/shard_map/finish/pallas_call | solution.py:668

commit v6 on v5

--- a/solution.py
+++ b/solution.py
@@ -160,10 +160,15 @@
         up = hop(src.at[1], dst.at[0], ssem.at[1], rsem.at[0], "tile", t + 1)
         return down, up
 
+    def tile_down(*refs):
+        pl.when(t > 0)(tile_pair(*refs)[0].start)
+
+    def tile_up(*refs):
+        pl.when(t < tiles - 1)(tile_pair(*refs)[1].start)
+
     def tile_start(src, dst, ssem, rsem):
-        down, up = tile_pair(src, dst, ssem, rsem)
-        pl.when(t > 0)(down.start)
-        pl.when(t < tiles - 1)(up.start)
+        tile_down(src, dst, ssem, rsem)
+        tile_up(src, dst, ssem, rsem)
 
     def tile_wait(src, dst, ssem, rsem):
         down, up = tile_pair(src, dst, ssem, rsem)
@@ -384,16 +389,15 @@
                         i, pl.ds(2 * (spare - r + at), STEP, stride=2), :
                     ]
 
-        lay(0, margin)
-        lay(n - margin, n)
-        add(0, margin)
-        add(margin + core, width)
-        if not isinstance(k, int):
-            @pl.when(k == ticks - 1)
-            def _():
-                edge_out[0] = total[0:margin, :].astype(BF16)
-                edge_out[1] = total[margin + core :, :].astype(BF16)
-                tile_start(edge_out, edge_in, send_e, recv_e)
+        final = None if isinstance(k, int) else k == ticks - 1
+        for side, lo, at, start in ((0, 0, 0, tile_down), (1, n - margin, margin + core, tile_up)):
+            lay(lo, lo + margin)
+            add(at, at + margin)
+            if final is not None:
+                @pl.when(final)
+                def _():
+                    edge_out[side] = total[at : at + margin, :].astype(BF16)
+                    start(edge_out, edge_in, send_e, recv_e)
         lay(margin, n - margin)
         add(margin, margin + core)
 
@@ -499,19 +503,20 @@
     pl.when(aside)(lambda: send_aside(0))
     for at, side, rows in strips:
         phase_table(at, halo_in[side, rows, :].astype(F32))
+    window_f(0)
+
+    @pl.when(jnp.logical_not(last))
+    def _():
+        forward(0, False)
+
+    @pl.when(last)
+    def _():
+        forward_last(0, False)
+
     window_b(0)
     for c in range(nc):
         rows = slice(c * ROWS, (c + 1) * ROWS)
         send_back(0, c, bk[0, rows, :], bk[1, rows, :])
-    window_f(0)
-
-    @pl.when(jnp.logical_not(last))
-    def _():
-        forward(0, False)
-
-    @pl.when(last)
-    def _():
-        forward_last(0, False)
 
     @pl.when(relay)
     def _():
@@ -523,30 +528,38 @@
         for k in range(1, ticks - 1):
             send_aside(k)
 
-    windows(1)
-    pl.when(relay)(lambda: side_phase(1))
+    early = jnp.logical_or(first, jnp.logical_and(odd, jnp.logical_not(last)))
     loads["saved"].wait()
-    scatter(0)
-
-    early = jnp.logical_or(first, jnp.logical_and(lax.rem(s, 2) == 1, jnp.logical_not(last)))
 
     @pl.when(early)
     def _():
+        window_f(1)
+
         def tick(k, carry):
             forward(k)
 
-            @pl.when(k < ticks - 1)
-            def _():
-                windows(k + 1)
-            pl.when(jnp.logical_and(relay, k < ticks - 2))(lambda: side_phase(k + 1))
+            @pl.when(k == 1)
+            def _():
+                window_b(1)
+                pl.when(relay)(lambda: side_phase(1))
+                scatter(0)
             backward(k)
             pl.when(jnp.logical_and(relay, k < ticks - 1))(lambda: pass_on(k))
             scatter(k)
+
+            @pl.when(k < ticks - 1)
+            def _():
+                windows(k + 1)
+            pl.when(jnp.logical_and(relay, k < ticks - 2))(lambda: side_phase(k + 1))
             return carry
         lax.fori_loop(1, ticks, tick, 0)
 
     @pl.when(jnp.logical_not(early))
     def _():
+        windows(1)
+        pl.when(relay)(lambda: side_phase(1))
+        scatter(0)
+
         def tick(k, carry):
             backward(k)
             pl.when(jnp.logical_and(relay, k < ticks - 1))(lambda: pass_on(k))

time: 24.3 us -> 23.3 us (0.959)
  Pallas kernels: 23.5 us -> 22.5 us
    pallas_call x1, Pallas kernels: 22.5 us -> 21.5 us  [on_device(): pl.pallas_call(functools.partial(kernel, sections, tiles), out_shape=(plt...]
where the time goes in v6:
time: 23.3 us; the launch traced here: 23.1 us
  Pallas kernels  22.5 us (97%)
  between operations  0.64 us (3%)
    pallas_call x1, Pallas kernels, on_device(): pl.pallas_call(functools.partial(kernel, sections, tiles), out_shape=(plt...  21.5 us
    pallas_call x1, Pallas kernels, on_device(): pl.pallas_call(finish, out_shape=(jax.ShapeDtypeStruct(fwd_wave.shape, F3...  1.03 us

profile of v6, /device:TPU:1, one launch (start us, length us, event | category | flops | bytes accessed | tf_op | source)
XLA Modules:
  0.0 23.1 jit_solution(17104437435221552606)
XLA Ops:
  0.6 21.5 %window.1 = (f32[1,1,2,256,256]{4,3,2,1,0:T(8,128)S(1)}, bf16[1,1,2,256,256]{4,3,2,1,0:T(8,128)(2,1)S(1)}, f32[1,256,384]{2,1,0:T(8,128)S(1)}) custom-call(s32[1,2,19]{2,1,0:T(2,128)} %bitcast.1, f32[1,256,384]{2,1,0:T(8,128)} %pot_h.1, bf16[2,256,256]{2,1,0:T(8,128)(2,1)} %probe_h.1, bf16[1,4,256,256]{3,2,1,0:T(8,128)(2,1)} %inten_h.1, ...), custom_call_target="tpu_custom_call" | custom-call | tf_op jit(solution)/shard_map/window/pallas_call | solution.py:651
  22.1 1.0 %finish.1 = (f32[1,1,2,256,256]{4,3,2,1,0:T(8,128)}, bf16[1,1,2,256,256]{4,3,2,1,0:T(8,128)(2,1)}, f32[1,256,384]{2,1,0:T(8,128)}) custom-call(f32[1,1,2,256,256]{4,3,2,1,0:T(8,128)S(1)} %get-tuple-element.6.wave, bf16[1,1,2,256,256]{4,3,2,1,0:T(8,128)(2,1)S(1)} %get-tuple-element.7.adj, f32[1,256,384]{2,1,0:T(8,128)S(1)} %get-tuple-element.8.grad), custom_call_target="tpu_custom_call" | custom-call | tf_op jit(solution)/shard_map/finish/pallas_call | solution.py:681

commit v7 on v6

--- a/solution.py
+++ b/solution.py
@@ -260,7 +260,7 @@
     spare = width - n
     for i in range(cols + 1):
         pad[i, 0 : 2 * spare, :] = jnp.zeros((2 * spare, LANES), F32)
-        pad[i, 2 * (spare + n) :, :] = jnp.zeros((2 * spare, LANES), F32)
+        pad[i, 2 * (spare + n) : 2 * (2 * spare + n), :] = jnp.zeros((2 * spare, LANES), F32)
     loads["fwd"].wait()
     for c in range(nc):
         rows = slice(c * ROWS, (c + 1) * ROWS)
@@ -660,8 +660,8 @@
         scratch_shapes=[
             wave(ticks + 1), wave(ticks + 1), wave(ticks), wave(ticks), wave(ticks - 1),
             held(main), lt, rt, lt, rt,
-            pltpu.VMEM((width // LANES, 3 * width, LANES), F32), pair, pair, pair, pltpu.VMEM((2, n, n), F32),
-            square, pltpu.VMEM((width // LANES, 4 * width - 2 * n, LANES), F32),
+            pltpu.VMEM((width // LANES, 3 * width + 8, LANES), F32), pair, pair, pair, pltpu.VMEM((2, n, n), F32),
+            square, pltpu.VMEM((width // LANES, 4 * width - 2 * n + 8, LANES), F32),
             pltpu.VMEM((nc, 2 * ROWS, n), BF16),
             strip, strip, strip, strip, view(nc), view(nc),
             view(ticks - 1, nc), view(ticks - 1, nc),

time: 23.3 us -> 23.4 us (level)
  no operation moved by 1% of the time
where the time goes in v7:
time: 23.4 us; the launch traced here: 23.2 us
  Pallas kernels  22.5 us (96%)
  between operations  0.64 us (3%)
    pallas_call x1, Pallas kernels, on_device(): pl.pallas_call(functools.partial(kernel, sections, tiles), out_shape=(plt...  21.5 us
    pallas_call x1, Pallas kernels, on_device(): pl.pallas_call(finish, out_shape=(jax.ShapeDtypeStruct(fwd_wave.shape, F3...  1.03 us

profile of v7, /device:TPU:1, one launch (start us, length us, event | category | flops | bytes accessed | tf_op | source)
XLA Modules:
  0.0 23.2 jit_solution(10046582987059901595)
XLA Ops:
  0.6 21.5 %window.1 = (f32[1,1,2,256,256]{4,3,2,1,0:T(8,128)S(1)}, bf16[1,1,2,256,256]{4,3,2,1,0:T(8,128)(2,1)S(1)}, f32[1,256,384]{2,1,0:T(8,128)S(1)}) custom-call(s32[1,2,19]{2,1,0:T(2,128)} %bitcast.1, f32[1,256,384]{2,1,0:T(8,128)} %pot_h.1, bf16[2,256,256]{2,1,0:T(8,128)(2,1)} %probe_h.1, bf16[1,4,256,256]{3,2,1,0:T(8,128)(2,1)} %inten_h.1, ...), custom_call_target="tpu_custom_call" | custom-call | tf_op jit(solution)/shard_map/window/pallas_call | solution.py:651
  22.1 1.0 %finish.1 = (f32[1,1,2,256,256]{4,3,2,1,0:T(8,128)}, bf16[1,1,2,256,256]{4,3,2,1,0:T(8,128)(2,1)}, f32[1,256,384]{2,1,0:T(8,128)}) custom-call(f32[1,1,2,256,256]{4,3,2,1,0:T(8,128)S(1)} %get-tuple-element.6.wave, bf16[1,1,2,256,256]{4,3,2,1,0:T(8,128)(2,1)S(1)} %get-tuple-element.7.adj, f32[1,256,384]{2,1,0:T(8,128)S(1)} %get-tuple-element.8.grad), custom_call_target="tpu_custom_call" | custom-call | tf_op jit(solution)/shard_map/finish/pallas_call | solution.py:681
